TPU v7x, 256 devices: a whole 4x4x8 slice. The times are simulated.
256 devices in a mesh: cells: 64 (over y, z, core), leaf: 4 (over x).
Axes of the slice: x: 4, y: 4, z: 8, core: 2. Of those that a mesh axis runs over, the one named last changes fastest.
Arguments:
- displacement: float32 [3, 119808], P(None, 'cells'), may hold values from -0.9 to 0.9
- point_leaf: int32 [119808], P('cells'), may hold values from 0 to 2047, as said below
- near_list: int32 [48, 2048], replicated, may hold values from -1 to 2047, as said below
- far_list: int32 [48, 2048], replicated, may hold values from -1 to 2047, as said below
- stiffness: float32 [312, 312], replicated, may hold values from -0.3125 to 0.3125
- up_inverse: float32 [168, 168], replicated, may hold values from -9 to 9
- down_inverse: float32 [168, 168], replicated, may hold values from -9 to 9
Outputs:
- velocity: float32 [3, 119808], P(None, 'cells')
Inputs may be any that keep to these rules, and one draw needn't show every extreme that they name: `point_leaf`: leaf L belongs to owner L // 32. All 312 points of one cell lie in at most three consecutive leaves of one owner, and that owner's index differs from the index of cells that holds the cell by at most one, cyclically (the last owner and owner 0 count as adjacent). Among the 1872 points of one index of cells, at most 936 lie in the leaves of one owner, and on every index some owner receives exactly 936. `near_list`: column L holds L itself and distinct leaves L' with |L' // 16 - L // 16| <= 1; the other entries are -1. `far_list`: column L holds distinct leaves L' with |L' // 16 - L // 16| >= 2, at least half the column, followed by -1 in the remaining entries.
All inputs are finite; a program needn't handle non-finite values.
Results may differ from a plain program's by a relative error of at most 0.0003.
Values sent between devices are 32-bit elements; how exact they have to be, the bound alone decides.
A program may use at most 64 MiB of HBM per device.

v0:
```python
import math

import jax
import jax.numpy as jnp
import numpy as np
from jax import lax
from jax.sharding import PartitionSpec as P

NPT = 312
SLICE = 16
EQUIV = 56
FAR = 48


inv_eight_pi = 1.0 / (8.0 * math.pi)
smooth_sq = 0.0625
inner_radius = 1.05
outer_radius = 2.95
highest = lax.Precision.HIGHEST


def from_behind(value, axis, steps):
    count = lax.axis_size(axis)
    pairs = [(source, (source + steps) % count) for source in range(count)]
    return lax.ppermute(value, axis, pairs)


def copy_for_each(array, axis):
    count = lax.axis_size(axis)
    return lax.all_to_all(
        jnp.broadcast_to(array[None], (count, *array.shape)), axis, 0, 0, tiled=True
    )


def laid_out(parts, dim):
    parts = jnp.moveaxis(parts, 0, dim)
    shape = parts.shape
    return parts.reshape(*shape[:dim], shape[dim] * shape[dim + 1], *shape[dim + 2 :])


def gathered_copies(array, axis, dim):
    parts = copy_for_each(array, axis)
    return laid_out(parts, dim)


def extended(block, sides, width):
    for axis, dim in sides:
        count = lax.axis_size(axis)
        forward = [(i, i + 1) for i in range(count - 1)]
        backward = [(target, source) for source, target in forward]
        low = lax.ppermute(
            lax.slice_in_dim(block, block.shape[dim] - width, None, axis=dim), axis, forward
        )
        high = lax.ppermute(lax.slice_in_dim(block, 0, width, axis=dim), axis, backward)
        block = jnp.concatenate([low, block, high], axis=dim)
    return block


def surface_table():
    ladder = [-1.0, -1.0 / 3.0, 1.0 / 3.0, 1.0]
    corners = [
        (xshift, yshift, zshift)
        for xshift in ladder
        for yshift in ladder
        for zshift in ladder
        if max(abs(xshift), abs(yshift), abs(zshift)) == 1.0
    ]
    return np.array(corners, dtype=np.float32).T


def leaf_centers(leaves):
    along = leaves // SLICE
    across = leaves % SLICE // 4
    height = leaves % 4
    return jnp.stack([2 * along + 1, 2 * across + 1, 2 * height + 1]).astype(jnp.float32)


def stokeslet(target, source, strength):
    offset = target - source
    radius_sq = jnp.sum(offset * offset, axis=0)
    inner = jnp.sum(offset * strength, axis=0)
    shifted = radius_sq + smooth_sq
    factor = inv_eight_pi * lax.rsqrt(shifted) / shifted
    return factor * ((radius_sq + 2.0 * smooth_sq) * strength + inner * offset)


def far_checks(gathered, sources, usable, column, first_leaf, surface):
    per_owner, listed = sources.shape
    pairs = per_owner * listed
    group = math.gcd(pairs, 96)
    target_slot = jnp.repeat(jnp.arange(per_owner, dtype=jnp.int32), listed)
    source_leaf = jnp.maximum(sources, 0).reshape(pairs)
    weights = (
        jnp.take(gathered, column.reshape(pairs), axis=1)
        * usable.reshape(pairs).astype(jnp.float32)[None, :]
    )
    strength = weights.reshape(3, EQUIV, pairs)
    check_mid = leaf_centers(first_leaf + target_slot)
    equiv_mid = leaf_centers(source_leaf)

    def one_group(index):
        start = index * group
        check = lax.dynamic_slice_in_dim(check_mid, start, group, 1)
        equiv = lax.dynamic_slice_in_dim(equiv_mid, start, group, 1)
        push = lax.dynamic_slice_in_dim(strength, start, group, 2)
        check_points = check[:, None, None, :] + inner_radius * surface[:, :, None, None]
        equiv_points = equiv[:, None, :] + inner_radius * surface[:, :, None]
        return jnp.sum(stokeslet(check_points, equiv_points[:, None], push[:, None]), axis=2)

    pieces = lax.map(one_group, jnp.arange(pairs // group, dtype=jnp.int32))
    pair_checks = jnp.transpose(pieces, (1, 2, 0, 3)).reshape(3 * EQUIV, pairs)
    pair_owner = (target_slot[:, None] == jnp.arange(per_owner, dtype=jnp.int32)[None, :]).astype(
        jnp.float32
    )
    return jnp.dot(pair_checks, pair_owner, precision=highest)


def body(displacement, point_leaf, near_list, far_list, stiffness, up_inverse, down_inverse):
    owners = lax.axis_size("cells")
    myself = lax.axis_index("cells")
    splits = lax.axis_size("leaf")
    portion = lax.axis_index("leaf")
    npoints = displacement.shape[1]
    capacity = npoints // NPT // 2 * NPT
    slots = 3 * capacity
    per_owner = 2 * SLICE
    rows_equiv = 3 * EQUIV
    surface = jnp.asarray(surface_table())
    membrane = displacement.reshape(3, npoints // NPT, NPT)
    forces = jnp.einsum("acn,nm->acm", membrane, stiffness, precision=highest).reshape(3, npoints)
    positions = leaf_centers(point_leaf) + displacement
    destination = point_leaf // per_owner
    lane = (destination - myself + 1 + owners) % owners
    lane_ids = jnp.arange(3, dtype=jnp.int32)
    onehot = (lane[:, None] == lane_ids[None, :]).astype(jnp.int32)
    ranking = jnp.sum((jnp.cumsum(onehot, axis=0) - 1) * onehot, axis=1)
    placed = lane * capacity + ranking
    labels = (point_leaf + 1).astype(jnp.float32)[None, :]
    packet = jnp.concatenate([positions, forces, labels], axis=0)
    outgoing = jnp.zeros((7, slots), jnp.float32).at[:, placed].set(packet)
    lanes_out = [outgoing[:, index * capacity : (index + 1) * capacity] for index in range(3)]
    received = {}
    for step_by, lane_index in ((1, 2), (-1, 0)):
        received[step_by] = from_behind(lanes_out[lane_index], "cells", step_by)
    arrived = jnp.concatenate([received[1], lanes_out[1], received[-1]], axis=1)
    recv_pos = arrived[0:3]
    recv_force = arrived[3:6]
    recv_leaf = arrived[6].astype(jnp.int32) - 1
    alive = recv_leaf >= 0
    recv_mid = leaf_centers(jnp.maximum(recv_leaf, 0))
    first_leaf = myself * per_owner
    own_slot = recv_leaf - first_leaf
    member = (
        (own_slot[:, None] == jnp.arange(per_owner, dtype=jnp.int32)[None, :]) & alive[:, None]
    ).astype(jnp.float32)
    check_up = recv_mid[:, None, :] + outer_radius * surface[:, :, None]
    upward_terms = stokeslet(check_up, recv_pos[:, None, :], recv_force[:, None, :]).reshape(
        rows_equiv, slots
    )
    upward = jnp.dot(upward_terms, member, precision=highest)
    density = jnp.dot(up_inverse, upward, precision=highest)
    far_rows = lax.dynamic_slice_in_dim(far_list, first_leaf, per_owner, 1).T
    gathered = gathered_copies(density, "cells", 1)
    share_rows = far_rows.reshape(per_owner, FAR // splits, splits)
    sources = lax.dynamic_index_in_dim(share_rows, portion, 2, keepdims=False)
    usable = sources >= 0
    column = jnp.maximum(sources, 0)
    downward_part = far_checks(gathered, sources, usable, column, first_leaf, surface)
    neighbours = extended(arrived, (("cells", 1),), slots)
    src_pos = neighbours[0:3]
    src_force = neighbours[3:6]
    src_leaf = neighbours[6].astype(jnp.int32) - 1
    span = 3 * per_owner
    span_ids = jnp.arange(span, dtype=jnp.int32)
    src_local = jnp.where(src_leaf >= 0, src_leaf - first_leaf + per_owner, span)
    src_member = (span_ids[:, None] == src_local[None, :]).astype(jnp.float32)
    near_rows = lax.dynamic_slice_in_dim(near_list, first_leaf, per_owner, 1).T
    near_local = jnp.where(near_rows >= 0, near_rows - first_leaf + per_owner, span)
    near_matrix = jnp.sum(
        (near_local[:, :, None] == span_ids[None, None, :]).astype(jnp.float32), axis=1
    )
    reach = jnp.dot(near_matrix, src_member, precision=highest)
    share = slots // splits
    block = max((candidate for candidate in range(1, 129) if share % candidate == 0))
    target_pos = lax.dynamic_slice_in_dim(recv_pos, portion * share, share, 1)
    target_member = lax.dynamic_slice_in_dim(member, portion * share, share, 0)

    def near_block(index):
        start = index * block
        points = lax.dynamic_slice_in_dim(target_pos, start, block, 1)
        belong = lax.dynamic_slice_in_dim(target_member, start, block, 0)
        weight = jnp.dot(belong, reach, precision=highest)
        pulls = stokeslet(points[:, :, None], src_pos[:, None, :], src_force[:, None, :])
        return jnp.sum(pulls * weight[None], axis=2)

    near_pieces = lax.map(near_block, jnp.arange(share // block, dtype=jnp.int32))
    near_share = jnp.transpose(near_pieces, (1, 0, 2)).reshape(3, share)
    near_full = lax.dynamic_update_slice_in_dim(
        jnp.zeros((3, slots), jnp.float32), near_share, portion * share, 1
    )
    near_all, downward = lax.psum((near_full, downward_part), "leaf")
    local = jnp.dot(down_inverse, downward, precision=highest)
    spread = jnp.dot(local, member.T, precision=highest).reshape(3, EQUIV, slots)
    equiv_down = recv_mid[:, None, :] + outer_radius * surface[:, :, None]
    far_velocity = jnp.sum(stokeslet(recv_pos[:, None, :], equiv_down, spread), axis=1)
    slot_velocity = (near_all + far_velocity) * alive.astype(jnp.float32)[None, :]
    lanes_back = [slot_velocity[:, index * capacity : (index + 1) * capacity] for index in range(3)]
    delivered = {}
    for step_by, lane_index in ((-1, 0), (1, 2)):
        delivered[step_by] = from_behind(lanes_back[lane_index], "cells", step_by)
    homeward = jnp.concatenate([delivered[1], lanes_back[1], delivered[-1]], axis=1)
    return homeward[:, placed]


def solution(mesh):
    in_specs = (P(None, "cells"), P("cells"), P(), P(), P(), P(), P())
    out_specs = P(None, "cells")
    return jax.shard_map(body, mesh=mesh, in_specs=in_specs, out_specs=out_specs, check_vma=False)
```

profile of v0, /device:TPU:1, one launch (start us, length us, event | category | flops | bytes accessed | tf_op | source)
XLA Modules:
  0.0 203.8 jit_solution(11728316923305395268)
XLA Ops:
  4.9 8.3 %scatter_custom_fusion = f32[7,2808]{0,1:T(8,128)S(1)} fusion(s32[1872]{0:T(1024)S(1)} %compare_select_fusion.4, f32[1872,7]{1,0:T(8,128)S(1)} %copy.49, f32[]{:T(128)} %constant.260.clone.1), kind=kCustom, calls=%fused_computation.63 | custom fusion | bytes 78628 | tf_op jit(solution)/shard_map/scatter | solution.py:140
  13.3 3.1 %collective-permute-start = (f32[7,936]{0,1:T(8,128)S(1)}, f32[7,936]{0,1:T(8,128)S(1)}, u32[]{:S(2)}, u32[]{:S(2)}) collective-permute-start(f32[7,936]{0,1:T(8,128)S(1)} %get-tuple-element.172), channel_id=1, source_target_pairs={{0,4},{4,8},{8,12},{12,16},{16,20},{20,24},{24,28},{28,32},{32,36}... | collective-permute-start | bytes 78632 | tf_op jit(solution)/shard_map/ppermute | solution.py:25
  25.4 2.9 %collective-permute-start.2 = (f32[7,2808]{1,0:T(8,128)S(1)}, f32[7,2808]{1,0:T(8,128)}, u32[]{:S(2)}, u32[]{:S(2)}) collective-permute-start(f32[7,2808]{1,0:T(8,128)S(1)} %concatenate.18), channel_id=1, source_target_pairs={{0,4},{4,8},{8,12},{12,16},{16,20},{20,24},{24,28},{28,32},{32,36}... | collective-permute-start | bytes 235880 | tf_op jit(solution)/shard_map/ppermute | solution.py:51
  28.4 6.5 %collective-permute-start.3 = (f32[7,2808]{1,0:T(8,128)S(1)}, f32[7,2808]{1,0:T(8,128)}, u32[]{:S(2)}, u32[]{:S(2)}) collective-permute-start(f32[7,2808]{1,0:T(8,128)S(1)} %concatenate.18), channel_id=1, source_target_pairs={{4,0},{8,4},{12,8},{16,12},{20,16},{24,20},{28,24},{32,28},{36,32}... | collective-permute-start | bytes 235880 | tf_op jit(solution)/shard_map/ppermute | solution.py:54
  36.8 2.0 fusion.31
  39.3 2.1 %fusion.64 = f32[168,32]{0,1:T(8,128)S(1)} fusion(f32[168,2808]{1,0:T(8,128)S(1)} %fusion.29, s32[2808]{0:T(1024)S(1)} %get-tuple-element.182, pred[2808]{0:T(1024)(128)(4,1)S(1)} %compare_reduce_fusion), kind=kOutput, calls=%fused_computation.188 | convolution fusion | flops 181329408 | bytes 1922520 | tf_op jit(solution)/shard_map/dot_general | solution.py:160
  43.2 10.0 %all-to-all-start = ((f32[64,168,32]{1,2,0:T(8,128)}), f32[64,168,32]{1,2,0:T(8,128)}, u32[]{:S(2)}, u32[]{:S(2)}) async-start(f32[64,168,32]{1,2,0:T(8,128)} %broadcast_in_dim.62), calls=%async_computation | async-start | bytes 4194304 | tf_op jit(solution)/shard_map/all_to_all | solution.py:30
  57.8 87.4 %while.21 = (s32[]{:T(128)}, f32[6,3,117]{2,1,0:T(4,128)}, s32[6]{0:T(128)}, f32[3,702]{1,0:T(4,128)}, f32[3,8424]{1,0:T(4,128)S(1)}, /*index=5*/f32[3,8424]{1,0...) while((s32[]{:T(128)}, f32[6,3,117]{2,1,0:T(4,128)}, ...), condition=%wide.region_9.10_spmd, body=%wide.region_5.9_spmd.sunk | while | flops 415926208 | bytes 40982620 | solution.py:196
  60.5 2.5 %fusion.91 = (f32[117,8424]{1,0:T(8,128)S(1)}, f32[117,8424]{1,0:T(8,128)S(1)}) fusion(f32[3,8424]{1,0:T(4,128)S(1)} %get-tuple-element.344, f32[3,117]{1,0:T(4,128)S(1)} %constant_dynamic-slice_fusion.10, f32[3,8424]{1,0:T(4,128)S(1)} %get-tuple-element.345), kind=kLoop, calls=%fused_computation.6.clone.1 | loop fusion | flops 12812904 | bytes 8088444 | tf_op jit(solution)/shard_map/while/body/eval_jaxpr/reduce_sum | solution.py:80
  64.1 3.3 %fusion.90 = f32[117,8424]{1,0:T(8,128)S(1)} fusion(f32[32,8424]{1,0:T(8,128)S(1)} %get-tuple-element.347, f32[702,32]{1,0:T(8,128)S(1)} %get-tuple-element.346, s32[]{:T(128)S(6)} %select_n.294), kind=kOutput, calls=%fused_computation.14.clone.1 | convolution fusion | flops 378473472 | bytes 5085220 | tf_op jit(solution)/shard_map/while/body/eval_jaxpr/dot_general | solution.py:192
  67.4 4.4 %fusion.92 = f32[3,117]{1,0:T(4,128)S(1)} fusion(f32[117,8424]{1,0:T(8,128)S(1)} %fusion.90, f32[117,8424]{1,0:T(8,128)S(1)} %get-tuple-element.298, f32[3,8424]{1,0:T(4,128)S(1)} %get-tuple-element.345, f32[117,8424]{1,0:T(8,128)S(1)} %get-tuple-element.300, f32[117,8424]{1,0:T(8,128)S(1)} %get-tuple-element.301, ...), kind=kLoop, calls=%fused_computation.11.clone.1 | loop fusion | flops 20697416 | bytes 15974712 | tf_op jit(solution)/shard_map/while/body/eval_jaxpr/reduce_sum | solution.py:194
  75.1 2.5 %fusion.91 = (f32[117,8424]{1,0:T(8,128)S(1)}, f32[117,8424]{1,0:T(8,128)S(1)}) fusion(f32[3,8424]{1,0:T(4,128)S(1)} %get-tuple-element.344, f32[3,117]{1,0:T(4,128)S(1)} %constant_dynamic-slice_fusion.10, f32[3,8424]{1,0:T(4,128)S(1)} %get-tuple-element.345), kind=kLoop, calls=%fused_computation.6.clone.1 | loop fusion | flops 12812904 | bytes 8088444 | tf_op jit(solution)/shard_map/while/body/eval_jaxpr/reduce_sum | solution.py:80
  78.7 3.3 %fusion.90 = f32[117,8424]{1,0:T(8,128)S(1)} fusion(f32[32,8424]{1,0:T(8,128)S(1)} %get-tuple-element.347, f32[702,32]{1,0:T(8,128)S(1)} %get-tuple-element.346, s32[]{:T(128)S(6)} %select_n.294), kind=kOutput, calls=%fused_computation.14.clone.1 | convolution fusion | flops 378473472 | bytes 5085220 | tf_op jit(solution)/shard_map/while/body/eval_jaxpr/dot_general | solution.py:192
  82.0 4.4 %fusion.92 = f32[3,117]{1,0:T(4,128)S(1)} fusion(f32[117,8424]{1,0:T(8,128)S(1)} %fusion.90, f32[117,8424]{1,0:T(8,128)S(1)} %get-tuple-element.298, f32[3,8424]{1,0:T(4,128)S(1)} %get-tuple-element.345, f32[117,8424]{1,0:T(8,128)S(1)} %get-tuple-element.300, f32[117,8424]{1,0:T(8,128)S(1)} %get-tuple-element.301, ...), kind=kLoop, calls=%fused_computation.11.clone.1 | loop fusion | flops 20697416 | bytes 15974712 | tf_op jit(solution)/shard_map/while/body/eval_jaxpr/reduce_sum | solution.py:194
  89.7 2.5 %fusion.91 = (f32[117,8424]{1,0:T(8,128)S(1)}, f32[117,8424]{1,0:T(8,128)S(1)}) fusion(f32[3,8424]{1,0:T(4,128)S(1)} %get-tuple-element.344, f32[3,117]{1,0:T(4,128)S(1)} %constant_dynamic-slice_fusion.10, f32[3,8424]{1,0:T(4,128)S(1)} %get-tuple-element.345), kind=kLoop, calls=%fused_computation.6.clone.1 | loop fusion | flops 12812904 | bytes 8088444 | tf_op jit(solution)/shard_map/while/body/eval_jaxpr/reduce_sum | solution.py:80
  93.2 3.3 %fusion.90 = f32[117,8424]{1,0:T(8,128)S(1)} fusion(f32[32,8424]{1,0:T(8,128)S(1)} %get-tuple-element.347, f32[702,32]{1,0:T(8,128)S(1)} %get-tuple-element.346, s32[]{:T(128)S(6)} %select_n.294), kind=kOutput, calls=%fused_computation.14.clone.1 | convolution fusion | flops 378473472 | bytes 5085220 | tf_op jit(solution)/shard_map/while/body/eval_jaxpr/dot_general | solution.py:192
  96.6 4.4 %fusion.92 = f32[3,117]{1,0:T(4,128)S(1)} fusion(f32[117,8424]{1,0:T(8,128)S(1)} %fusion.90, f32[117,8424]{1,0:T(8,128)S(1)} %get-tuple-element.298, f32[3,8424]{1,0:T(4,128)S(1)} %get-tuple-element.345, f32[117,8424]{1,0:T(8,128)S(1)} %get-tuple-element.300, f32[117,8424]{1,0:T(8,128)S(1)} %get-tuple-element.301, ...), kind=kLoop, calls=%fused_computation.11.clone.1 | loop fusion | flops 20697416 | bytes 15974712 | tf_op jit(solution)/shard_map/while/body/eval_jaxpr/reduce_sum | solution.py:194
  104.2 2.5 %fusion.91 = (f32[117,8424]{1,0:T(8,128)S(1)}, f32[117,8424]{1,0:T(8,128)S(1)}) fusion(f32[3,8424]{1,0:T(4,128)S(1)} %get-tuple-element.344, f32[3,117]{1,0:T(4,128)S(1)} %constant_dynamic-slice_fusion.10, f32[3,8424]{1,0:T(4,128)S(1)} %get-tuple-element.345), kind=kLoop, calls=%fused_computation.6.clone.1 | loop fusion | flops 12812904 | bytes 8088444 | tf_op jit(solution)/shard_map/while/body/eval_jaxpr/reduce_sum | solution.py:80
  107.8 3.3 %fusion.90 = f32[117,8424]{1,0:T(8,128)S(1)} fusion(f32[32,8424]{1,0:T(8,128)S(1)} %get-tuple-element.347, f32[702,32]{1,0:T(8,128)S(1)} %get-tuple-element.346, s32[]{:T(128)S(6)} %select_n.294), kind=kOutput, calls=%fused_computation.14.clone.1 | convolution fusion | flops 378473472 | bytes 5085220 | tf_op jit(solution)/shard_map/while/body/eval_jaxpr/dot_general | solution.py:192
  111.1 4.4 %fusion.92 = f32[3,117]{1,0:T(4,128)S(1)} fusion(f32[117,8424]{1,0:T(8,128)S(1)} %fusion.90, f32[117,8424]{1,0:T(8,128)S(1)} %get-tuple-element.298, f32[3,8424]{1,0:T(4,128)S(1)} %get-tuple-element.345, f32[117,8424]{1,0:T(8,128)S(1)} %get-tuple-element.300, f32[117,8424]{1,0:T(8,128)S(1)} %get-tuple-element.301, ...), kind=kLoop, calls=%fused_computation.11.clone.1 | loop fusion | flops 20697416 | bytes 15974712 | tf_op jit(solution)/shard_map/while/body/eval_jaxpr/reduce_sum | solution.py:194
  118.8 2.5 %fusion.91 = (f32[117,8424]{1,0:T(8,128)S(1)}, f32[117,8424]{1,0:T(8,128)S(1)}) fusion(f32[3,8424]{1,0:T(4,128)S(1)} %get-tuple-element.344, f32[3,117]{1,0:T(4,128)S(1)} %constant_dynamic-slice_fusion.10, f32[3,8424]{1,0:T(4,128)S(1)} %get-tuple-element.345), kind=kLoop, calls=%fused_computation.6.clone.1 | loop fusion | flops 12812904 | bytes 8088444 | tf_op jit(solution)/shard_map/while/body/eval_jaxpr/reduce_sum | solution.py:80
  122.4 3.3 %fusion.90 = f32[117,8424]{1,0:T(8,128)S(1)} fusion(f32[32,8424]{1,0:T(8,128)S(1)} %get-tuple-element.347, f32[702,32]{1,0:T(8,128)S(1)} %get-tuple-element.346, s32[]{:T(128)S(6)} %select_n.294), kind=kOutput, calls=%fused_computation.14.clone.1 | convolution fusion | flops 378473472 | bytes 5085220 | tf_op jit(solution)/shard_map/while/body/eval_jaxpr/dot_general | solution.py:192
  125.7 4.4 %fusion.92 = f32[3,117]{1,0:T(4,128)S(1)} fusion(f32[117,8424]{1,0:T(8,128)S(1)} %fusion.90, f32[117,8424]{1,0:T(8,128)S(1)} %get-tuple-element.298, f32[3,8424]{1,0:T(4,128)S(1)} %get-tuple-element.345, f32[117,8424]{1,0:T(8,128)S(1)} %get-tuple-element.300, f32[117,8424]{1,0:T(8,128)S(1)} %get-tuple-element.301, ...), kind=kLoop, calls=%fused_computation.11.clone.1 | loop fusion | flops 20697416 | bytes 15974712 | tf_op jit(solution)/shard_map/while/body/eval_jaxpr/reduce_sum | solution.py:194
  133.3 2.5 %fusion.91 = (f32[117,8424]{1,0:T(8,128)S(1)}, f32[117,8424]{1,0:T(8,128)S(1)}) fusion(f32[3,8424]{1,0:T(4,128)S(1)} %get-tuple-element.344, f32[3,117]{1,0:T(4,128)S(1)} %constant_dynamic-slice_fusion.10, f32[3,8424]{1,0:T(4,128)S(1)} %get-tuple-element.345), kind=kLoop, calls=%fused_computation.6.clone.1 | loop fusion | flops 12812904 | bytes 8088444 | tf_op jit(solution)/shard_map/while/body/eval_jaxpr/reduce_sum | solution.py:80
  136.9 3.3 %fusion.90 = f32[117,8424]{1,0:T(8,128)S(1)} fusion(f32[32,8424]{1,0:T(8,128)S(1)} %get-tuple-element.347, f32[702,32]{1,0:T(8,128)S(1)} %get-tuple-element.346, s32[]{:T(128)S(6)} %select_n.294), kind=kOutput, calls=%fused_computation.14.clone.1 | convolution fusion | flops 378473472 | bytes 5085220 | tf_op jit(solution)/shard_map/while/body/eval_jaxpr/dot_general | solution.py:192
  140.2 4.4 %fusion.92 = f32[3,117]{1,0:T(4,128)S(1)} fusion(f32[117,8424]{1,0:T(8,128)S(1)} %fusion.90, f32[117,8424]{1,0:T(8,128)S(1)} %get-tuple-element.298, f32[3,8424]{1,0:T(4,128)S(1)} %get-tuple-element.345, f32[117,8424]{1,0:T(8,128)S(1)} %get-tuple-element.300, f32[117,8424]{1,0:T(8,128)S(1)} %get-tuple-element.301, ...), kind=kLoop, calls=%fused_computation.11.clone.1 | loop fusion | flops 20697416 | bytes 15974712 | tf_op jit(solution)/shard_map/while/body/eval_jaxpr/reduce_sum | solution.py:194
  146.4 3.4 %gather_fusion = f32[384,168]{1,0:T(8,128)S(1)} fusion(f32[168,2048]{0,1:T(8,128)} %bitcast.16, s32[1024]{0:T(1024)} %pad_clamp_fusion.1), kind=kCustom, calls=%fused_computation | custom fusion | bytes 517632 | tf_op jit(solution)/shard_map/jit(_take)/gather | solution.py:94
  150.0 22.0 %while.22 = (s32[]{:T(128)}, f32[4,3,56,96]{3,2,1,0:T(8,128)S(1)}, s32[4]{0:T(128)S(1)}, f32[3,384]{1,0:T(4,128)}, f32[3,384]{1,0:T(4,128)}, /*index=5*/f32[3,56...) while((s32[]{:T(128)}, f32[4,3,56,96]{3,2,1,0:T(8,128)S(1)}, ...), condition=%wide.region_18.19_spmd.clone, body=%wide.region_14.18_spmd.sunk.clone.sunk | while | flops 10553094 | bytes 10523219 | solution.py:110
  172.8 14.2 %all-reduce.1 = (f32[3,2808]{1,0:T(4,128)S(1)}, f32[168,32]{0,1:T(8,128)S(1)}) all-reduce(f32[3,2808]{1,0:T(4,128)S(1)} %dynamic_update_slice.11, f32[168,32]{0,1:T(8,128)S(1)} %fusion.36), channel_id=1, replica_groups=mesh['cells'=64,'leaf'=4] {'leaf'}, use_global_device_ids=true, to_apply=%region_10.11 | all-reduce | flops 13800 | bytes 110400 | tf_op jit(solution)/shard_map/psum | solution.py:201
  190.3 5.4 %collective-permute-start.4 = (f32[3,936]{1,0:T(4,128)S(1)}, f32[3,936]{1,0:T(4,128)S(1)}, u32[]{:S(2)}, u32[]{:S(2)}) collective-permute-start(f32[3,936]{1,0:T(4,128)S(1)} %get-tuple-element.187), channel_id=1, source_target_pairs={{0,4},{4,8},{8,12},{12,16},{16,20},{20,24},{24,28},{28,32},{32,36}... | collective-permute-start | bytes 33704 | tf_op jit(solution)/shard_map/ppermute | solution.py:25
  196.6 2.3 %collective-permute-done.5 = f32[3,936]{1,0:T(4,128)S(1)} collective-permute-done((f32[3,936]{1,0:T(4,128)S(1)}, f32[3,936]{1,0:T(4,128)S(1)}, u32[]{:S(2)}, u32[]{:S(2)}) %collective-permute-start.5) | collective-permute-done | bytes 11264 | tf_op jit(solution)/shard_map/ppermute | solution.py:25
  199.4 3.4 %gather_fusion.1 = f32[1872,3]{1,0:T(8,128)S(1)} fusion(f32[3,2808]{0,1:T(8,128)S(1)} %copy.61, s32[2048]{0:T(1024)S(1)} %pad_clamp_fusion), kind=kCustom, calls=%fused_computation.1 | custom fusion | bytes 52416 | tf_op jit(solution)/shard_map/gather | solution.py:212
  (199 shorter events, 71.2 us)
Async XLA Ops:
  0.0 3.2 %copy-start = (f32[312,312]{1,0:T(8,128)S(1)}, f32[312,312]{1,0:T(8,128)}, u32[]{:S(2)}) copy-start(f32[312,312]{1,0:T(8,128)} %param.16) | copy-start | bytes 1168132
  2.3 2.6 %copy-start.14 = (s32[1872]{0:T(1024)}, s32[1872]{0:T(1024)S(1)}, u32[]{:S(2)}) copy-start(s32[1872]{0:T(1024)S(1)} %compare_select_fusion.4) | copy-start | bytes 22468
  13.3 21.6 %copy-start.16 = (f32[3,56]{1,0:T(4,128)S(1)}, f32[3,56]{1,0:T(4,128)}, u32[]{:S(2)}) copy-start(f32[3,56]{1,0:T(4,128)} %constant.295) | copy-start | bytes 2020
  13.3 10.8 %collective-permute-start = (f32[7,936]{0,1:T(8,128)S(1)}, f32[7,936]{0,1:T(8,128)S(1)}, u32[]{:S(2)}, u32[]{:S(2)}) collective-permute-start(f32[7,936]{0,1:T(8,128)S(1)} %get-tuple-element.172), channel_id=1, source_target_pairs={{0,4},{4,8},{8,12},{12,16},{16,20},{20,24},{24,28},{28,32},{32,36}... | collective-permute-start | bytes 78632 | tf_op jit(solution)/shard_map/ppermute | solution.py:25
  16.4 8.4 %collective-permute-start.1 = (f32[7,936]{0,1:T(8,128)S(1)}, f32[7,936]{0,1:T(8,128)S(1)}, u32[]{:S(2)}, u32[]{:S(2)}) collective-permute-start(f32[7,936]{0,1:T(8,128)S(1)} %get-tuple-element.170), channel_id=1, source_target_pairs={{0,252},{4,0},{8,4},{12,8},{16,12},{20,16},{24,20},{28,24},{32,28}... | collective-permute-start | bytes 78632 | tf_op jit(solution)/shard_map/ppermute | solution.py:25
  22.2 13.5 %copy-start.2 = (f32[7,936]{1,0:T(8,128)}, f32[7,936]{1,0:T(8,128)S(1)}, u32[]{:S(2)}) copy-start(f32[7,936]{1,0:T(8,128)S(1)} %copy.51) | copy-start | bytes 78628
  24.4 10.5 %copy-start.4 = (f32[7,936]{1,0:T(8,128)}, f32[7,936]{1,0:T(8,128)S(1)}, u32[]{:S(2)}) copy-start(f32[7,936]{1,0:T(8,128)S(1)} %copy.50) | copy-start | bytes 78628
  25.0 9.9 %copy-start.6 = (f32[7,936]{1,0:T(8,128)}, f32[7,936]{1,0:T(8,128)S(1)}, u32[]{:S(2)}) copy-start(f32[7,936]{1,0:T(8,128)S(1)} %copy.52) | copy-start | bytes 78628
  25.4 13.8 %copy-start.10 = (pred[2808]{0:T(1024)(128)(4,1)}, pred[2808]{0:T(1024)(128)(4,1)S(1)}, u32[]{:S(2)}) copy-start(pred[2808]{0:T(1024)(128)(4,1)S(1)} %compare_reduce_fusion) | copy-start | bytes 8428
  25.4 28.6 %collective-permute-start.2 = (f32[7,2808]{1,0:T(8,128)S(1)}, f32[7,2808]{1,0:T(8,128)}, u32[]{:S(2)}, u32[]{:S(2)}) collective-permute-start(f32[7,2808]{1,0:T(8,128)S(1)} %concatenate.18), channel_id=1, source_target_pairs={{0,4},{4,8},{8,12},{12,16},{16,20},{20,24},{24,28},{28,32},{32,36}... | collective-permute-start | bytes 235880 | tf_op jit(solution)/shard_map/ppermute | solution.py:51
  28.4 25.6 %collective-permute-start.3 = (f32[7,2808]{1,0:T(8,128)S(1)}, f32[7,2808]{1,0:T(8,128)}, u32[]{:S(2)}, u32[]{:S(2)}) collective-permute-start(f32[7,2808]{1,0:T(8,128)S(1)} %concatenate.18), channel_id=1, source_target_pairs={{4,0},{8,4},{12,8},{16,12},{20,16},{24,20},{28,24},{32,28},{36,32}... | collective-permute-start | bytes 235880 | tf_op jit(solution)/shard_map/ppermute | solution.py:54
  36.1 2.7 %copy-start.21 = (f32[168]{0:T(256)S(1)}, f32[168]{0:T(256)}, u32[]{:S(2)}) copy-start(f32[168]{0:T(256)} %constant.296) | copy-start | bytes 2020
  39.2 2.1 %copy-start.8 = (f32[168,168]{1,0:T(8,128)S(1)}, f32[168,168]{1,0:T(8,128)}, u32[]{:S(2)}) copy-start(f32[168,168]{1,0:T(8,128)} %param.17) | copy-start | bytes 338692
  43.2 10.8 %copy-start.3 = (f32[7,936]{1,0:T(8,128)S(1)}, f32[7,936]{1,0:T(8,128)}, u32[]{:S(2)}) copy-start(f32[7,936]{1,0:T(8,128)} %copy-done.2) | copy-start | bytes 78628
  43.2 10.8 %copy-start.5 = (f32[7,936]{1,0:T(8,128)S(1)}, f32[7,936]{1,0:T(8,128)}, u32[]{:S(2)}) copy-start(f32[7,936]{1,0:T(8,128)} %copy-done.4) | copy-start | bytes 78628
  43.2 10.8 %copy-start.7 = (f32[7,936]{1,0:T(8,128)S(1)}, f32[7,936]{1,0:T(8,128)}, u32[]{:S(2)}) copy-start(f32[7,936]{1,0:T(8,128)} %copy-done.6) | copy-start | bytes 78628
  43.2 103.2 %all-to-all-start = ((f32[64,168,32]{1,2,0:T(8,128)}), f32[64,168,32]{1,2,0:T(8,128)}, u32[]{:S(2)}, u32[]{:S(2)}) async-start(f32[64,168,32]{1,2,0:T(8,128)} %broadcast_in_dim.62), calls=%async_computation | async-start | bytes 4194304 | tf_op jit(solution)/shard_map/all_to_all | solution.py:30
  145.2 4.7 %copy-start.19 = (f32[384]{0:T(512)S(1)}, f32[384]{0:T(512)}, u32[]{:S(2)}) copy-start(f32[384]{0:T(512)} %reshape.536) | copy-start | bytes 4612
  145.2 4.8 %copy-start.20 = (pred[384]{0:T(512)(128)(4,1)S(1)}, pred[384]{0:T(512)(128)(4,1)}, u32[]{:S(2)}) copy-start(pred[384]{0:T(512)(128)(4,1)} %le.16) | copy-start | bytes 1156
  145.2 4.8 %copy-start.1 = (f32[4,3,56,96]{3,2,1,0:T(8,128)S(1)}, f32[4,3,56,96]{3,2,1,0:T(8,128)}, u32[]{:S(2)}) copy-start(f32[4,3,56,96]{3,2,1,0:T(8,128)} %custom-call.5) | copy-start | bytes 774148
  145.2 4.8 %copy-start.12 = (f32[3,56]{1,0:T(4,128)S(1)}, f32[3,56]{1,0:T(4,128)}, u32[]{:S(2)}) copy-start(f32[3,56]{1,0:T(4,128)} %constant.441) | copy-start | bytes 2020
  150.0 22.3 %copy-start.18 = (s32[384]{0:T(512)S(1)}, s32[384]{0:T(512)}, u32[]{:S(2)}) copy-start(s32[384]{0:T(512)} %eq.104) | copy-start | bytes 4612
  150.0 36.9 %copy-start.9 = (f32[168,168]{1,0:T(8,128)S(1)}, f32[168,168]{1,0:T(8,128)}, u32[]{:S(2)}) copy-start(f32[168,168]{1,0:T(8,128)} %param.18) | copy-start | bytes 338692
  172.0 15.2 %copy-start.11 = (pred[2808]{0:T(1024)(128)(4,1)S(1)}, pred[2808]{0:T(1024)(128)(4,1)}, u32[]{:S(2)}) copy-start(pred[2808]{0:T(1024)(128)(4,1)} %copy-done.10) | copy-start | bytes 8428
  172.0 17.0 %copy-start.17 = (f32[3,56]{1,0:T(4,128)S(1)}, f32[3,56]{1,0:T(4,128)}, u32[]{:S(2)}) copy-start(f32[3,56]{1,0:T(4,128)} %constant.295) | copy-start | bytes 2020
  189.4 0.7 copy-start.13
  189.5 6.2 %copy-start.15 = (s32[1872]{0:T(1024)S(1)}, s32[1872]{0:T(1024)}, u32[]{:S(2)}) copy-start(s32[1872]{0:T(1024)} %copy-done.14) | copy-start | bytes 22468
  190.3 6.3 %collective-permute-start.4 = (f32[3,936]{1,0:T(4,128)S(1)}, f32[3,936]{1,0:T(4,128)S(1)}, u32[]{:S(2)}, u32[]{:S(2)}) collective-permute-start(f32[3,936]{1,0:T(4,128)S(1)} %get-tuple-element.187), channel_id=1, source_target_pairs={{0,4},{4,8},{8,12},{12,16},{16,20},{20,24},{24,28},{28,32},{32,36}... | collective-permute-start | bytes 33704 | tf_op jit(solution)/shard_map/ppermute | solution.py:25
  195.7 3.2 %collective-permute-start.5 = (f32[3,936]{1,0:T(4,128)S(1)}, f32[3,936]{1,0:T(4,128)S(1)}, u32[]{:S(2)}, u32[]{:S(2)}) collective-permute-start(f32[3,936]{1,0:T(4,128)S(1)} %get-tuple-element.185), channel_id=1, source_target_pairs={{0,252},{4,0},{8,4},{12,8},{16,12},{20,16},{24,20},{28,24},{32,28}... | collective-permute-start | bytes 33704 | tf_op jit(solution)/shard_map/ppermute | solution.py:25
where the time goes:
time: 205 us; the launch traced here: 204 us
  other arithmetic  72.8 us (36%)
  local copies, waits for them, and re-layouts  50 us (24%)
  starting transfers between devices  28.3 us (14%)
  matrix products  27.2 us (13%)
  blocking collectives  14.2 us (7%)
  loops' own time  7.08 us (3%)
  waiting for transfers between devices  3.64 us (2%)
    reduce_sum x6, other arithmetic, near_block(): return jnp.sum(pulls * weight[None], axis=2)  26.3 us
    reduce_sum x11, other arithmetic, stokeslet(): radius_sq = jnp.sum(offset * offset, axis=0)  20.5 us
    dot_general x6, matrix products, near_block(): weight = jnp.dot(belong, reach, precision=highest)  20 us
    psum x1, blocking collectives, body(): near_all, downward = lax.psum((near_full, downward_part), 'leaf')  14.2 us
    all_to_all x1, starting transfers between devices, copy_for_each(): lax.all_to_all(jnp.broadcast_to(array[None], (count, *array.shape)), axis...  10 us
    ppermute x4, starting transfers between devices, from_behind(): return lax.ppermute(value, axis, pairs)  8.81 us
    div x11, other arithmetic, stokeslet(): factor = inv_eight_pi * lax.rsqrt(shifted) / shifted  8.38 us
    scatter x1, local copies, waits for them, and re-layouts, body(): outgoing = jnp.zeros((7, slots), jnp.float32).at[:, placed].set(packet)  8.33 us
  transfers between devices with their start and end apart: 7, of which 3 were waited for; matrix products, arithmetic and copies ran while one was open for 51% of the time, Pallas kernels for 0%

commit v1 on v0

v1 whole, which is shorter than its diff:
```python
import math

import jax
import jax.numpy as jnp
import numpy as np
from jax import lax
from jax.experimental import pallas as pl
from jax.experimental.pallas import tpu as pltpu
from jax.sharding import PartitionSpec as P

NPT = 312
CPD = 6
SLICE = 16
EQUIV = 56
FAR = 48
ROWS = 3 * EQUIV
PER_OWNER = 2 * SLICE
WIDE = 384
OFFSETS = (1, -1, 2, -2, 3, -3)
CELLS = CPD * (len(OFFSETS) + 1)
OWNABLE = 3 * CPD
SHARE = NPT // 4
SHARE_PAD = 80
COUNT = 127

inv_eight_pi = 1.0 / (8.0 * math.pi)
smooth_sq = 0.0625
inner_radius = 1.05
outer_radius = 2.95
MESH = pl.DeviceIdType.MESH
VMEM = pl.BlockSpec(memory_space=pltpu.VMEM)
SMEM = pl.BlockSpec(memory_space=pltpu.SMEM)
f32 = jnp.float32
bf16 = jnp.bfloat16
i32 = jnp.int32


def surface_table():
    ladder = [-1.0, -1.0 / 3.0, 1.0 / 3.0, 1.0]
    corners = [
        (a, b, c)
        for a in ladder
        for b in ladder
        for c in ladder
        if max(abs(a), abs(b), abs(c)) == 1.0
    ]
    return np.array(corners, dtype=np.float32)


def iota(shape, dim):
    return lax.broadcasted_iota(i32, shape, dim)


def dot(a, b):
    return jnp.dot(a, b, preferred_element_type=f32)


def dot_nt(a, b):
    return lax.dot_general(a, b, (((1,), (1,)), ((), ())), preferred_element_type=f32)


def halves(value):
    top = value.astype(bf16)
    return top, (value - top.astype(f32)).astype(bf16)


def dot_wide(a, b):
    a_top, a_low = halves(a)
    b_top, b_low = halves(b)
    return dot(a_top, b_top) + (dot(a_top, b_low) + dot(a_low, b_top))


DX, DY, DZ, FX, FY, FZ, PX, PY, PZ, REL = range(10)
FEATURES = 24
DEPTH = FEATURES + 8 * CPD
FAR_AWAY = 1e30
DUMMY = CELLS
BATCH = 3


def thirds(value):
    top = value.astype(bf16).astype(f32)
    rest = value - top
    middle = rest.astype(bf16).astype(f32)
    return top, middle, rest - middle


def pull(offset, strength):
    dx, dy, dz = offset
    fx, fy, fz = strength
    shifted = (dx * dx + dy * dy) + (dz * dz + smooth_sq)
    inner = (dx * fx + dy * fy) + dz * fz
    root = lax.rsqrt(shifted)
    cube = root * root * root
    return root + smooth_sq * cube, cube * inner


def remote(src, dst, send_sem, recv_sem, target):
    return pltpu.make_async_remote_copy(
        src_ref=src,
        dst_ref=dst,
        send_sem=send_sem,
        recv_sem=recv_sem,
        device_id=target,
        device_id_type=MESH,
    )


def greet(targets):
    barrier = pltpu.get_barrier_semaphore()
    for target in targets:
        pl.semaphore_signal(barrier, inc=1, device_id=target, device_id_type=MESH)
    pl.semaphore_wait(barrier, len(targets))


def beside(axis, offsets):
    count = lax.axis_size(axis)
    me = lax.axis_index(axis)
    return [{axis: lax.rem(me + (off + count), count)} for off in offsets]


def first_kernel(
    disp_ref,
    leaf_ref,
    near_ref,
    stiff_ref,
    surf_ref,
    inverse_ref,
    comp_ref,
    lists_ref,
    gat_ref,
    wanted_ref,
    lefts_ref,
    spots_ref,
    held_disp,
    held_leaf,
    disp,
    leaves,
    force,
    listed_ref,
    relation,
    wide,
    terms_top,
    terms_low,
    member_ref,
    total,
    density,
    block_ref,
    send_disp,
    recv_disp,
    send_leaf,
    recv_leaf,
    own_sem,
    z_send,
    z_recv,
    y_send,
    y_recv,
    c_send,
    c_recv,
):
    me = lax.axis_index("cells")
    portion = lax.axis_index("leaf")
    core = lax.rem(me, 2)
    z = lax.rem(me // 2, 8)
    y = me // 16

    def device(y_at, z_at, core_at):
        return {"cells": (y_at * 8 + z_at) * 2 + core_at}

    sides = beside("cells", OFFSETS)
    z_targets = [device(y, lax.rem(z + k, 8), core) for k in range(1, 8)]
    y_targets = [device(lax.rem(y + k, 4), z, core) for k in range(1, 4)]
    c_target = device(y, z, 1 - core)
    greet([*sides, *z_targets, *y_targets, c_target])
    copies = []
    for slot, target in enumerate(sides):
        copies.append(
            remote(disp_ref, held_disp.at[slot], send_disp.at[slot], recv_disp.at[slot], target)
        )
        copies.append(
            remote(leaf_ref, held_leaf.at[slot], send_leaf.at[slot], recv_leaf.at[slot], target)
        )
    for copy in copies:
        copy.start()

    comp_ref[...] = jnp.zeros_like(comp_ref)
    disp[...] = jnp.zeros_like(disp)
    leaves[...] = jnp.zeros_like(leaves)

    def place_cells(home, points, leaf_row):
        for k in range(CPD):
            at = slice(NPT * k, NPT * (k + 1))
            row = home * CPD + k
            for a in range(3):
                disp[48 * a + row : 48 * a + row + 1, 0:NPT] = points[a : a + 1, at]
            leaves[row : row + 1, 0:NPT] = leaf_row[:, at]

    def fill_table(rows):
        live = iota((rows, WIDE), 1) < NPT
        rel = jnp.where(live, (leaves[0:rows, :] - PER_OWNER * (me - 4)) & 2047, -1)
        for a in range(3):
            comp_ref[DX + a, 0:rows, :] = disp[48 * a : 48 * a + rows, :]
        comp_ref[REL, 0:rows, :] = rel.astype(f32)
        comp_ref[PX, 0:rows, :] = comp_ref[DX, 0:rows, :] + (2 * (rel >> 4) + 1).astype(f32)
        comp_ref[PY, 0:rows, :] = comp_ref[DY, 0:rows, :] + (2 * ((rel >> 2) & 3) + 1).astype(f32)
        comp_ref[PZ, 0:rows, :] = comp_ref[DZ, 0:rows, :] + (2 * (rel & 3) + 1).astype(f32)
        relf = rel.astype(f32)
        first = jnp.min(jnp.where(live, relf, 1e9), axis=1, keepdims=True)
        last = jnp.max(relf, axis=1, keepdims=True)
        return first, last

    place_cells(0, disp_ref[...], leaf_ref[...])
    first, last = fill_table(8)

    start = lax.rem(me + 63, 64)
    block = start // 4
    left = near_ref[:, pl.ds(pl.multiple_of(block * 128, 128), 128)]
    right = near_ref[:, pl.ds(pl.multiple_of(lax.rem(block + 1, 16) * 128, 128), 128)]
    both = jnp.concatenate([left, right], axis=1)
    listed = both[:, 0:128]
    for k in range(1, 4):
        listed = jnp.where(lax.rem(start, 4) == k, both[:, 32 * k : 32 * k + 128], listed)
    listed_ref[...] = jnp.where(listed >= 0, (listed - PER_OWNER * (me - 2)) & 2047, -1)
    source_leaf = iota((160, 128), 0)

    def eight_entries(index, near):
        rows = listed_ref[pl.ds(pl.multiple_of(8 * index, 8), 8), :]
        for k in range(8):
            near = near + jnp.where(rows[k : k + 1, :] == source_leaf, 1.0, 0.0)
        return near

    near = lax.fori_loop(0, 6, eight_entries, jnp.zeros((160, 128), f32))
    relation[...] = near.astype(bf16)
    row8, lane8 = iota((8, 128), 0).astype(f32), iota((8, 128), 1).astype(f32)
    leaf_rows = [
        jnp.where((lane8 == first[t : t + 1] - 3.0 * PER_OWNER + row8) & (row8 < 3.0), 1.0, 0.0)
        for t in range(CPD)
    ]
    wanted_ref[...] = dot_nt(jnp.concatenate(leaf_rows, axis=0).astype(bf16), relation[...])

    pick_row, pick_lane = iota((SHARE_PAD, WIDE), 0), iota((SHARE_PAD, WIDE), 1)
    pick16 = ((pick_lane == pick_row + SHARE * portion) & (pick_row < SHARE)).astype(f32).astype(bf16)
    slot = iota((SHARE_PAD, 128), 1)
    slot_turn = lax.rem(slot, 6)
    left_first = (slot < 18) & (slot_turn < 3) | (slot == 18)
    left_second = (slot < 18) & (slot_turn >= 3) & (slot_turn < 5) | (slot == 19)
    row32 = iota((32, WIDE), 0)

    def one_own(t, carry):
        rel = comp_ref[REL, pl.ds(t, 1), :]
        px, py, pz = [comp_ref[PX + a, pl.ds(t, 1), :] for a in range(3)]
        lowest = jnp.min(jnp.where(rel >= 0.0, rel, 1e9), axis=1, keepdims=True)
        owner = jnp.floor(lowest * (1.0 / PER_OWNER))
        py4, pz4 = py - 4.0, pz - 4.0
        extra = iota((8, WIDE), 0)
        place = jnp.where(extra == 0, px, jnp.where(extra == 1, py, jnp.where(extra == 2, pz, rel)))
        top, middle, low = thirds(place)
        spot = dot_nt(pick16, top.astype(bf16)) + (
            dot_nt(pick16, middle.astype(bf16)) + dot_nt(pick16, low.astype(bf16))
        )
        for a in range(3):
            spots_ref[t, a] = jnp.broadcast_to(spot[:, a : a + 1], (SHARE_PAD, 128))
        leaf_at = (spot[:, 3:4] - lowest).astype(i32)
        matched = (slot - (FEATURES + 8 * t) == leaf_at) & (leaf_at >= 0) & (leaf_at < 3)
        for w in range(3):
            px4 = px - (4.0 * (owner + float(w - 1)) + 2.0)
            square = (px4 * px4 + py4 * py4) + pz4 * pz4
            rows = jnp.where(
                row32 < 6,
                px4,
                jnp.where(row32 < 12, py4, jnp.where(row32 < 18, pz4, square)),
            )
            rows = jnp.concatenate([rows, jnp.zeros((96, WIDE), f32)], axis=0)
            top, middle, low = thirds(rows)
            value = dot_nt(pick16, top.astype(bf16)) + (
                dot_nt(pick16, middle.astype(bf16)) + dot_nt(pick16, low.astype(bf16))
            )
            top, middle, low = thirds(value)
            chosen = jnp.where(left_first, top, jnp.where(left_second, middle, low))
            chosen = jnp.where((slot >= 21) & (slot < 24), 1.0, chosen)
            chosen = jnp.where(slot >= FEATURES, jnp.where(matched, 1.0, 0.0), chosen)
            lefts_ref[3 * t + w] = chosen[:, 0:DEPTH].astype(bf16)
        return carry

    lax.fori_loop(0, CPD, one_own, 0)
    for a in range(3):
        wide[a] = jnp.broadcast_to(outer_radius * surf_ref[:, a : a + 1], (EQUIV, 128))

    for copy in copies:
        copy.wait()
    for home in range(1, len(OFFSETS) + 1):
        place_cells(home, held_disp[home - 1], held_leaf[home - 1])
    first, last = fill_table(48)
    force[...] = dot_wide(disp[0:144, 0:NPT], stiff_ref[...])
    for a in range(3):
        comp_ref[FX + a, 0:48, 0:NPT] = force[48 * a : 48 * a + 48, :]

    total[...] = jnp.zeros_like(total)

    def one_home(home, carry):
        for k in range(CPD):
            c = CPD * home + k
            d = [comp_ref[DX + a, pl.ds(c, 1), :] for a in range(3)]
            f = [comp_ref[FX + a, pl.ds(c, 1), :] for a in range(3)]
            rel = comp_ref[REL, pl.ds(c, 1), :].astype(i32) - 4 * PER_OWNER
            member = (iota((PER_OWNER, WIDE), 0) == rel).astype(f32).astype(bf16)
            member_ref[:, WIDE * k : WIDE * (k + 1)] = member
            for b in range(WIDE // 128):
                lanes = slice(128 * b, 128 * b + 128)
                out = slice(WIDE * k + 128 * b, WIDE * k + 128 * b + 128)
                for g in range(EQUIV // 8):
                    at = slice(8 * g, 8 * g + 8)
                    r = [wide[a, at, :] - d[a][:, lanes] for a in range(3)]
                    fb = [f[a][:, lanes] for a in range(3)]
                    even, along = pull(r, fb)
                    for a in range(3):
                        row = EQUIV * a + 8 * g
                        top, low = halves(even * fb[a] + along * r[a])
                        terms_top[row : row + 8, out] = top
                        terms_low[row : row + 8, out] = low
        total[...] += dot_nt(terms_top[...], member_ref[...]) + dot_nt(terms_low[...], member_ref[...])
        return carry

    lax.fori_loop(0, 3, one_home, 0)
    density[...] = dot_wide(inverse_ref[...], total[...] * inv_eight_pi)
    block_ref[...] = jnp.zeros_like(block_ref)
    for part in range(4):

        @pl.when(portion == part)
        def _():
            for a in range(3):
                rows = density[EQUIV * a + 14 * part : EQUIV * a + 14 * part + 14, :]
                block_ref[0:14, PER_OWNER * a : PER_OWNER * (a + 1)] = rows

    row = core * 4 + y
    own = pltpu.make_async_copy(block_ref, gat_ref.at[row, z], own_sem)
    own.start()
    z_copies = [
        remote(block_ref, gat_ref.at[row, z], z_send.at[k], z_recv.at[k], target)
        for k, target in enumerate(z_targets)
    ]
    for copy in z_copies:
        copy.start()

    low = jnp.floor(first * (1.0 / 16.0))
    high = jnp.floor(last * (1.0 / 16.0))
    lane = iota((48, 128), 1)
    which = iota((48, 1), 0).astype(f32)
    real = which < float(CELLS)
    flags = []
    for t in range(CPD):
        low_t, high_t = low[t : t + 1], high[t : t + 1]
        flags.append(jnp.where((high >= low_t - 1.0) & (low <= high_t + 1.0) & real, 1.0, 0.0))
    owner = jnp.floor(low * 0.5)
    union = flags[0]
    for t in range(1, CPD):
        union = jnp.maximum(union, flags[t])
    flags.append(union)
    table = jnp.zeros((48, 128), f32)
    for t, flag in enumerate(flags):
        table = table + jnp.where(lane == t, flag, 0.0)
    before = (iota((48, 48), 0) > iota((48, 48), 1)).astype(f32)
    rank = dot(before, table)
    count = jnp.sum(table, axis=0, keepdims=True)
    lane_row = iota((1, 128), 1)
    lists_ref[...] = jnp.zeros_like(lists_ref)
    for t, flag in enumerate(flags):
        hit = (rank[:, t : t + 1] == lane.astype(f32)) & (flag > 0.0)
        line = jnp.sum(jnp.where(hit, which, 0.0), axis=0, keepdims=True)
        line = jnp.where(lane_row.astype(f32) >= count[:, t : t + 1], float(DUMMY), line)
        line = jnp.where(lane_row == COUNT, count[:, t : t + 1], line)
        lists_ref[t : t + 1, :] = line.astype(i32)
    square = iota((48, 128), 0) == lane
    line = jnp.sum(jnp.where(square, owner, 0.0), axis=0, keepdims=True)
    lists_ref[7:8, :] = line.astype(i32)

    own.wait()
    for copy in z_copies:
        copy.wait()
    y_copies = [
        remote(gat_ref.at[row], gat_ref.at[row], y_send.at[k], y_recv.at[k], target)
        for k, target in enumerate(y_targets)
    ]
    for copy in y_copies:
        copy.start()
    c_copies = []
    for k in range(4):
        at = core * 4 + lax.rem(y - k + 4, 4)
        if k:
            y_copies[k - 1].wait_recv()
        copy = remote(gat_ref.at[at], gat_ref.at[at], c_send.at[k], c_recv.at[k], c_target)
        copy.start()
        c_copies.append(copy)
    for copy in y_copies:
        copy.wait_send()
    for copy in c_copies:
        copy.wait()


def first(displacement, leaf_row, near_list, stiffness, surf, up_inverse):
    npoints = displacement.shape[1]
    sides = len(OFFSETS)
    dma = pltpu.SemaphoreType.DMA
    return pl.pallas_call(
        first_kernel,
        out_shape=(
            jax.ShapeDtypeStruct((10, 48, WIDE), f32),
            jax.ShapeDtypeStruct((8, 128), i32),
            jax.ShapeDtypeStruct((8, 8, 16, 128), f32),
            jax.ShapeDtypeStruct((8 * CPD, 160), f32),
            jax.ShapeDtypeStruct((3 * CPD, SHARE_PAD, DEPTH), bf16),
            jax.ShapeDtypeStruct((CPD, 3, SHARE_PAD, 128), f32),
        ),
        in_specs=[VMEM] * 6,
        out_specs=(VMEM,) * 6,
        scratch_shapes=[
            pltpu.VMEM((sides, 3, npoints), f32),
            pltpu.VMEM((sides, 1, npoints), i32),
            pltpu.VMEM((144, WIDE), f32),
            pltpu.VMEM((48, WIDE), i32),
            pltpu.VMEM((144, NPT), f32),
            pltpu.VMEM((FAR, 128), i32),
            pltpu.VMEM((160, 128), bf16),
            pltpu.VMEM((3, EQUIV, 128), f32),
            pltpu.VMEM((ROWS, CPD * WIDE), bf16),
            pltpu.VMEM((ROWS, CPD * WIDE), bf16),
            pltpu.VMEM((PER_OWNER, CPD * WIDE), bf16),
            pltpu.VMEM((ROWS, PER_OWNER), f32),
            pltpu.VMEM((ROWS, PER_OWNER), f32),
            pltpu.VMEM((16, 128), f32),
            dma((sides,)),
            dma((sides,)),
            dma((sides,)),
            dma((sides,)),
            dma,
            dma((7,)),
            dma((7,)),
            dma((3,)),
            dma((3,)),
            dma((4,)),
            dma((4,)),
        ],
        compiler_params=pltpu.CompilerParams(collective_id=0, has_side_effects=True),
        name="first",
    )(displacement, leaf_row, near_list, stiffness, surf, up_inverse)


def near_kernel(
    lists, comp_ref, wanted_ref, lefts, spots, out_ref, rights, even_pairs, odd_pairs, sums
):
    portion = lax.axis_index("leaf")
    wanted = wanted_ref[...].astype(bf16)
    feature = iota((FEATURES, WIDE), 0)
    turn = lax.rem(feature, 6)
    first = (feature < 18) & ((turn == 0) | (turn == 3) | (turn == 5)) | (feature == 21)
    second = (feature < 18) & ((turn == 1) | (turn == 4)) | (feature == 22)

    def factors(x, y, z, last):
        value = jnp.where(
            feature < 6, x, jnp.where(feature < 12, y, jnp.where(feature < 18, z, last))
        )
        top, middle, low = thirds(value)
        return jnp.where(first, top, jnp.where(second, middle, low))

    def some_sources(index, carry):
        cells = [lists[6, BATCH * index + k] for k in range(BATCH)]
        rels = [comp_ref[REL, pl.ds(c, 1), :].astype(i32) for c in cells]
        hits = [
            (iota((160, WIDE), 0) == rel - 2 * PER_OWNER).astype(f32).astype(bf16) for rel in rels
        ]
        reaches = [dot(wanted, hit) for hit in hits]
        for k, c in enumerate(cells):
            rel = rels[k]
            px = comp_ref[PX, pl.ds(c, 1), :] - (4 * (rel >> 5) + 2).astype(f32)
            py = comp_ref[PY, pl.ds(c, 1), :] - 4.0
            pz = comp_ref[PZ, pl.ds(c, 1), :] - 4.0
            fx, fy, fz = [comp_ref[FX + a, pl.ds(c, 1), :] for a in range(3)]
            square = (px * px + py * py) + (pz * pz + smooth_sq)
            along = (px * fx + py * fy) + pz * fz
            near_rows = factors(-2.0 * px, -2.0 * py, -2.0 * pz, square)
            near_rows = jnp.where((feature >= 18) & (feature < 21), 1.0, near_rows)
            push_rows = factors(fx, fy, fz, -along)
            push_rows = jnp.where((feature >= 18) & (feature < 21), 0.0, push_rows)
            mask_rows = FAR_AWAY - FAR_AWAY * reaches[k]
            rights[c, :, 0:WIDE] = jnp.concatenate([near_rows, mask_rows], axis=0).astype(bf16)
            rights[c, 0:FEATURES, WIDE : 2 * WIDE] = push_rows.astype(bf16)
            rights[c, FEATURES:DEPTH, WIDE : 2 * WIDE] = jnp.zeros((8 * CPD, WIDE), bf16)
        return carry

    lax.fori_loop(0, (lists[6, COUNT] + (BATCH - 1)) // BATCH, some_sources, 0)
    rights[DUMMY] = jnp.where(iota((DEPTH, 2 * WIDE), 0) == 21, FAR_AWAY, 0.0).astype(bf16)

    def multiply(t, index, products):
        c = lists[t, index]
        w = jnp.clip(lists[7, c] - lists[7, t] + 1, 0, 2)
        products[...] = dot(lefts[3 * t + w], rights[c])

    def add_pair(t, index, products):
        c = lists[t, index]
        p = [comp_ref[PX + a, pl.ds(c, 1), :] for a in range(3)]
        f = [comp_ref[FX + a, pl.ds(c, 1), :] for a in range(3)]
        for g in range(SHARE_PAD // 8):
            at = slice(8 * g, 8 * g + 8)
            added = None
            for b in range(WIDE // 128):
                lanes = slice(128 * b, 128 * b + 128)
                shifted = products[at, lanes]
                inner = products[at, WIDE + 128 * b : WIDE + 128 * b + 128]
                root = lax.rsqrt(shifted)
                cube = root * root * root
                even = root + smooth_sq * cube
                along = cube * inner
                part = [even * f[a][:, lanes] - along * p[a][:, lanes] for a in range(3)]
                part.append(along)
                if added is None:
                    added = part
                else:
                    added = [u + v for u, v in zip(added, part)]
            for a in range(4):
                sums[a, at, :] += added[a]

    pick_row, pick_lane = iota((SHARE_PAD, WIDE), 0), iota((SHARE_PAD, WIDE), 1)
    pick = (pick_lane == pick_row + SHARE * portion) & (pick_row < SHARE)

    def one_target(t, carry):
        sums[...] = jnp.zeros_like(sums)
        multiply(t, 0, even_pairs)

        def two_pairs(index, carry):
            multiply(t, 2 * index + 1, odd_pairs)
            add_pair(t, 2 * index, even_pairs)
            multiply(t, 2 * index + 2, even_pairs)
            add_pair(t, 2 * index + 1, odd_pairs)
            return carry

        lax.fori_loop(0, (lists[t, COUNT] + 1) // 2, two_pairs, 0)
        for a in range(3):
            total = sums[a] + spots[t, a] * sums[3]
            column = jnp.sum(total, axis=1, keepdims=True) * inv_eight_pi
            row = jnp.sum(jnp.where(pick, column, 0.0), axis=0, keepdims=True)
            out_ref[a, pl.ds(t, 1), :] = row
        return carry

    lax.fori_loop(0, CPD, one_target, 0)


def near_field(lists, comp, wanted, lefts, spots):
    return pl.pallas_call(
        near_kernel,
        out_shape=jax.ShapeDtypeStruct((3, 8, WIDE), f32),
        in_specs=[SMEM] + [VMEM] * 4,
        out_specs=VMEM,
        scratch_shapes=[
            pltpu.VMEM((CELLS + 1, DEPTH, 2 * WIDE), bf16),
            pltpu.VMEM((SHARE_PAD, 2 * WIDE), f32),
            pltpu.VMEM((SHARE_PAD, 2 * WIDE), f32),
            pltpu.VMEM((4, SHARE_PAD, 128), f32),
        ],
        name="near_field",
    )(lists, comp, wanted, lefts, spots)


def far_part(
    points, gat_ref, far_ref, surf_ref, inverse_ref, local_ref, far4, sources, packed, pushes, mids, total
):
    me = lax.axis_index("cells")
    portion = lax.axis_index("leaf")
    lane = iota((16, 128), 1)

    def one_tile(tile, carry):
        for half in range(2):
            rows = [jnp.zeros((16, 128), f32) for _ in range(3)]
            for v in range(4):
                at = 8 * tile + 4 * half + v
                value = gat_ref[at // 8, at - at // 8 * 8]
                for a in range(3):
                    shift = (PER_OWNER * (v - a)) % 128
                    moved = pltpu.roll(value, shift, 1) if shift else value
                    rows[a] = jnp.where(lane // PER_OWNER == v, moved, rows[a])
            top, low = halves(jnp.concatenate(rows, axis=0))
            packed[tile, 0:48, 128 * half : 128 * half + 128] = top
            packed[tile, 48:96, 128 * half : 128 * half + 128] = low
        return carry

    lax.fori_loop(0, 8, one_tile, 0)

    block = pl.multiple_of(me // 4 * 128, 128)
    entries = far_ref[:, pl.ds(block, 128)]
    mine = lax.rem(me, 4)
    lane48 = iota((FAR, 128), 1) // PER_OWNER
    picked = jnp.zeros((FAR, 128), i32)
    for place in range(4):
        moved = entries
        for k in range(1, 4):
            turned = pltpu.roll(entries, PER_OWNER * k, 1)
            moved = jnp.where(lax.rem(mine + k, 4) == place, turned, moved)
        far4[place] = moved
    for place in range(4):
        rows = far4[place, pl.ds(place, FAR // 4, stride=4), :]
        chosen = iota((FAR // 4, 128), 1) // PER_OWNER == place
        if place == 0:
            merged = rows
        else:
            merged = jnp.where(chosen, rows, merged)
    owner = merged >> 5
    spot = (((owner & 1) << 5) + (owner >> 1)) * PER_OWNER + (merged & 31)
    sources[0:12, :] = jnp.where(merged >= 0, spot, -1)
    target = me * PER_OWNER + (iota((12, 128), 1) & 31)
    mids[0, 0:12, :] = (2 * ((target >> 4) - (merged >> 4))).astype(f32)
    mids[1, 0:12, :] = (2 * (((target >> 2) & 3) - ((merged >> 2) & 3))).astype(f32)
    mids[2, 0:12, :] = (2 * ((target & 3) - (merged & 3))).astype(f32)

    def one_gather(index, carry):
        first = sources[pl.ds(2 * index, 1), :]
        second = sources[pl.ds(2 * index + 1, 1), :]
        wanted = jnp.concatenate([first, second], axis=1)
        found = jnp.zeros((96, 256), f32)
        for tile in range(8):
            onehot = (iota((256, 256), 0) + 256 * tile == wanted).astype(f32).astype(bf16)
            found = found + dot(packed[tile], onehot)
        value = found[0:48] + found[48:96]
        pushes[2 * index] = value[:, 0:128]
        pushes[2 * index + 1] = value[:, 128:256]
        return carry

    lax.fori_loop(0, 6, one_gather, 0)
    total[...] = jnp.zeros_like(total)

    def one_block(index, carry):
        mid = [mids[a, pl.ds(index, 1), :] for a in range(3)]
        for g in range(EQUIV // 8):
            at = slice(8 * g, 8 * g + 8)
            check = [mid[a] + inner_radius * surf_ref[at, a : a + 1] for a in range(3)]
            sums = [total[EQUIV * a + 8 * g : EQUIV * a + 8 * g + 8, :] for a in range(3)]
            for j in range(14):
                f = [pushes[index, 16 * a + j : 16 * a + j + 1, :] for a in range(3)]
                r = [check[a] - points[3 * (14 * portion + j) + a] for a in range(3)]
                even, along = pull(r, f)
                sums = [sums[a] + (even * f[a] + along * r[a]) for a in range(3)]
            for a in range(3):
                total[EQUIV * a + 8 * g : EQUIV * a + 8 * g + 8, :] = sums[a]
        return carry

    lax.fori_loop(0, 12, one_block, 0)
    value = total[...] * inv_eight_pi
    value = value + pltpu.roll(value, 64, 1)
    value = value + pltpu.roll(value, 32, 1)
    local_ref[...] = dot_wide(inverse_ref[...], value)


def last_kernel(
    points,
    gat_ref,
    far_ref,
    surf_ref,
    inverse_ref,
    comp_ref,
    near_ref,
    out_ref,
    far4,
    sources,
    packed,
    pushes,
    mids,
    total,
    local_ref,
    held_local,
    factors,
    spread_ref,
    part_ref,
    held_part,
    send_local,
    recv_local,
    send_part,
    recv_part,
):
    sides = beside("cells", (1, -1))
    mates = beside("leaf", (1, 2, 3))
    barrier = pltpu.get_barrier_semaphore()
    for target in (*sides, *mates):
        pl.semaphore_signal(barrier, inc=1, device_id=target, device_id_type=MESH)
    far_part(
        points, gat_ref, far_ref, surf_ref, inverse_ref, local_ref, far4, sources, packed, pushes, mids, total
    )
    pl.semaphore_wait(barrier, 5)
    copies = [
        remote(local_ref, held_local.at[k], send_local.at[k], recv_local.at[k], target)
        for k, target in enumerate(sides)
    ]
    for copy in copies:
        copy.start()
    for copy in copies:
        copy.wait()
    lane = iota((ROWS, 128), 1) // PER_OWNER
    value = jnp.where(
        lane == 0, held_local[0], jnp.where(lane == 1, local_ref[...], held_local[1])
    )
    top, low = halves(value)
    factors[0:ROWS, :] = top
    factors[ROWS : 2 * ROWS, :] = low

    def one_cell(t, carry):
        rel = comp_ref[REL, pl.ds(t, 1), :].astype(i32) - 3 * PER_OWNER
        member = (iota((128, WIDE), 0) == rel).astype(f32).astype(bf16)
        both = dot(factors[...], member)
        spread_ref[t] = both[0:ROWS] + both[ROWS : 2 * ROWS]
        return carry

    lax.fori_loop(0, CPD, one_cell, 0)
    for t in range(CPD):
        d = [comp_ref[DX + a, t : t + 1, :] for a in range(3)]
        sums = [jnp.zeros((8, WIDE), f32) for _ in range(3)]
        for g in range(EQUIV // 8):
            at = slice(8 * g, 8 * g + 8)
            r = [d[a] - outer_radius * surf_ref[at, a : a + 1] for a in range(3)]
            f = [spread_ref[t, EQUIV * a + 8 * g : EQUIV * a + 8 * g + 8, :] for a in range(3)]
            even, along = pull(r, f)
            sums = [sums[a] + (even * f[a] + along * r[a]) for a in range(3)]
        for a in range(3):
            row = jnp.sum(sums[a], axis=0, keepdims=True) * inv_eight_pi + near_ref[a, t : t + 1, :]
            part_ref[a : a + 1, NPT * t : NPT * (t + 1)] = row[:, 0:NPT]
    copies = [
        remote(part_ref, held_part.at[k], send_part.at[k], recv_part.at[k], target)
        for k, target in enumerate(mates)
    ]
    for copy in copies:
        copy.start()
    for copy in copies:
        copy.wait()
    out_ref[...] = (part_ref[...] + held_part[1]) + (held_part[0] + held_part[2])


def last(points, gathered, far_list, surf, down_inverse, comp, near, npoints):
    dma = pltpu.SemaphoreType.DMA
    return pl.pallas_call(
        last_kernel,
        out_shape=jax.ShapeDtypeStruct((3, npoints), f32),
        in_specs=[SMEM] + [VMEM] * 6,
        out_specs=VMEM,
        scratch_shapes=[
            pltpu.VMEM((4, FAR, 128), i32),
            pltpu.VMEM((16, 128), i32),
            pltpu.VMEM((8, 96, 256), bf16),
            pltpu.VMEM((12, FAR, 128), f32),
            pltpu.VMEM((3, 16, 128), f32),
            pltpu.VMEM((ROWS, 128), f32),
            pltpu.VMEM((ROWS, 128), f32),
            pltpu.VMEM((2, ROWS, 128), f32),
            pltpu.VMEM((2 * ROWS, 128), bf16),
            pltpu.VMEM((CPD, ROWS, WIDE), f32),
            pltpu.VMEM((3, npoints), f32),
            pltpu.VMEM((3, 3, npoints), f32),
            dma((2,)),
            dma((2,)),
            dma((3,)),
            dma((3,)),
        ],
        compiler_params=pltpu.CompilerParams(collective_id=1, has_side_effects=True),
        name="last",
    )(points, gathered, far_list, surf, down_inverse, comp, near)


def body(displacement, point_leaf, near_list, far_list, stiffness, up_inverse, down_inverse):
    table = surface_table()
    surf = jnp.asarray(np.pad(table, ((0, 0), (0, 5))))
    points = jnp.asarray((inner_radius * table).astype(np.float32).reshape(-1))
    comp, lists, gathered, wanted, lefts, spots = first(
        displacement, point_leaf[None, :], near_list, stiffness, surf, up_inverse
    )
    near = near_field(lists, comp, wanted, lefts, spots)
    return last(
        points, gathered, far_list, surf, down_inverse, comp, near, displacement.shape[1]
    )


def solution(mesh):
    in_specs = (P(None, "cells"), P("cells"), P(), P(), P(), P(), P())
    out_specs = P(None, "cells")
    return jax.shard_map(body, mesh=mesh, in_specs=in_specs, out_specs=out_specs, check_vma=False)
```

time: 205 us -> 74.8 us (0.36)
  the two profiles are of different devices: /device:TPU:1 before, /device:TPU:8 now
where the time goes in v1:
time: 74.8 us; the launch traced here: 74.4 us
  Pallas kernels  71.7 us (96%)
  local copies, waits for them, and re-layouts  2.66 us (4%)
    pallas_call x1, Pallas kernels, first(): pl.pallas_call(first_kernel, out_shape=(jax.ShapeDtypeStruct((10, 48, WID...  30.2 us
    pallas_call x1, Pallas kernels, last(): pl.pallas_call(last_kernel, out_shape=jax.ShapeDtypeStruct((3, npoints),...  25.5 us
    pallas_call x1, Pallas kernels, near_field(): pl.pallas_call(near_kernel, out_shape=jax.ShapeDtypeStruct((3, 8, WIDE),...  16 us

profile of v1, /device:TPU:8, one launch (start us, length us, event | category | flops | bytes accessed | tf_op | source)
XLA Modules:
  0.0 74.4 jit_solution(3577085231405285570)
XLA Ops:
  0.0 1.3 %broadcast_in_dim.3.leaf_ref = s32[1,1872]{1,0:T(1,128)} reshape(s32[1872]{0:T(1024)} %param.10) | data formatting | bytes 14976 | tf_op jit(solution)/shard_map/broadcast_in_dim | solution.py:768
  1.3 30.2 %first.1 = (f32[10,48,384]{2,1,0:T(8,128)}, s32[8,128]{1,0:T(8,128)}, f32[8,8,16,128]{3,2,1,0:T(8,128)}, f32[48,160]{1,0:T(8,128)}, bf16[18,80,72]{2,1,0:T(8,128)(2,1)}, /*index=5*/f32[6,3,80,128]{3,2,1,0:T(8,128)}) custom-call(f32[3,1872]{1,0:T(4,128)} %disp_ref.1, s32[1,1872]{1,0:T(1,128)} %broadcast_in_dim.3.leaf_ref, s32[48,2048]{1,0:T(8,128)} %near_ref.1, ...), custom_call_target="tpu_custom_call" | custom-call | tf_op jit(solution)/shard_map/first/pallas_call | solution.py:404
  31.5 16.0 %near_field.1.near_ref = f32[3,8,384]{2,1,0:T(8,128)} custom-call(s32[8,128]{1,0:T(8,128)} %get-tuple-element.13.lists, f32[10,48,384]{2,1,0:T(8,128)} %get-tuple-element.12.comp_ref, f32[48,160]{1,0:T(8,128)} %get-tuple-element.14.wanted_ref, bf16[18,80,72]{2,1,0:T(8,128)(2,1)} %get-tuple-element.15.lefts, f32[6,3,80,128]{3,2,1,0:T(8,128)} %get-tuple-element.16.spots), custom_call_target="tpu_custom_call" | custom-call | tf_op jit(solution)/shard_map/near_field/pallas_call | solution.py:548
  47.5 25.5 %last.1 = f32[3,1872]{1,0:T(4,128)} custom-call(f32[168]{0:T(256)} %constant.5.clone.points, f32[8,8,16,128]{3,2,1,0:T(8,128)} %get-tuple-element.11.gat_ref, s32[48,2048]{1,0:T(8,128)} %far_ref.1, f32[56,8]{1,0:T(8,128)} %constant.4.clone.surf_ref, f32[168,168]{1,0:T(8,128)} %inverse_ref.3, f32[10,48,384]{2,1,0:T(8,128)} %get-tuple-element.12.comp_ref, ...), custom_call_target="tpu_custom_call" | custom-call | tf_op jit(solution)/shard_map/last/pallas_call | solution.py:735
  73.0 1.4 %copy.11 = f32[3,1872]{1,0:T(4,128)} copy(f32[3,1872]{1,0:T(4,128)} %last.1) | data formatting | bytes 44928

commit v2 on v1

--- a/solution.py
+++ b/solution.py
@@ -74,8 +74,11 @@
 FEATURES = 24
 DEPTH = FEATURES + 8 * CPD
 FAR_AWAY = 1e30
+LIMIT = 20 << 20
+HBM = pl.BlockSpec(memory_space=pltpu.HBM)
 DUMMY = CELLS
 BATCH = 3
+EARLY = 7
 
 
 def thirds(value):
@@ -93,6 +96,10 @@
     root = lax.rsqrt(shifted)
     cube = root * root * root
     return root + smooth_sq * cube, cube * inner
+
+
+def in_hbm(array):
+    return pltpu.with_memory_space_constraint(array, pltpu.HBM)
 
 
 def remote(src, dst, send_sem, recv_sem, target):
@@ -120,25 +127,32 @@
 
 
 def first_kernel(
+    disp_hbm,
+    leaf_hbm,
+    near_hbm,
+    stiff_hbm,
+    surf_hbm,
+    inverse_hbm,
+    comp_ref,
+    lists_ref,
+    gat_ref,
+    lefts_ref,
+    spots_ref,
+    rights_ref,
+    held_disp,
+    held_leaf,
     disp_ref,
+    surf_ref,
     leaf_ref,
     near_ref,
     stiff_ref,
-    surf_ref,
     inverse_ref,
-    comp_ref,
-    lists_ref,
-    gat_ref,
-    wanted_ref,
-    lefts_ref,
-    spots_ref,
-    held_disp,
-    held_leaf,
     disp,
     leaves,
     force,
     listed_ref,
     relation,
+    wanted_ref,
     wide,
     terms_top,
     terms_low,
@@ -150,6 +164,7 @@
     recv_disp,
     send_leaf,
     recv_leaf,
+    load_sem,
     own_sem,
     z_send,
     z_recv,
@@ -160,6 +175,25 @@
 ):
     me = lax.axis_index("cells")
     portion = lax.axis_index("leaf")
+    start = lax.rem(me + 63, 64)
+    block = start // 4
+    leaf_load = pltpu.make_async_copy(leaf_hbm, leaf_ref.at[0], load_sem.at[0])
+    loads = [
+        pltpu.make_async_copy(
+            near_hbm.at[:, pl.ds(pl.multiple_of(lax.rem(block + k, 16) * 128, 128), 128)],
+            near_ref.at[k],
+            load_sem.at[1 + k],
+        )
+        for k in range(2)
+    ]
+    loads.append(pltpu.make_async_copy(stiff_hbm, stiff_ref, load_sem.at[3]))
+    loads.append(pltpu.make_async_copy(inverse_hbm, inverse_ref, load_sem.at[4]))
+    loads.append(pltpu.make_async_copy(surf_hbm, surf_ref, load_sem.at[5]))
+    disp_load = pltpu.make_async_copy(disp_hbm, disp_ref, load_sem.at[6])
+    disp_load.start()
+    leaf_load.start()
+    for load in loads:
+        load.start()
     core = lax.rem(me, 2)
     z = lax.rem(me // 2, 8)
     y = me // 16
@@ -172,6 +206,8 @@
     y_targets = [device(lax.rem(y + k, 4), z, core) for k in range(1, 4)]
     c_target = device(y, z, 1 - core)
     greet([*sides, *z_targets, *y_targets, c_target])
+    disp_load.wait()
+    leaf_load.wait()
     copies = []
     for slot, target in enumerate(sides):
         copies.append(
@@ -212,11 +248,9 @@
     place_cells(0, disp_ref[...], leaf_ref[...])
     first, last = fill_table(8)
 
-    start = lax.rem(me + 63, 64)
-    block = start // 4
-    left = near_ref[:, pl.ds(pl.multiple_of(block * 128, 128), 128)]
-    right = near_ref[:, pl.ds(pl.multiple_of(lax.rem(block + 1, 16) * 128, 128), 128)]
-    both = jnp.concatenate([left, right], axis=1)
+    for load in loads:
+        load.wait()
+    both = jnp.concatenate([near_ref[0], near_ref[1]], axis=1)
     listed = both[:, 0:128]
     for k in range(1, 4):
         listed = jnp.where(lax.rem(start, 4) == k, both[:, 32 * k : 32 * k + 128], listed)
@@ -236,7 +270,9 @@
         jnp.where((lane8 == first[t : t + 1] - 3.0 * PER_OWNER + row8) & (row8 < 3.0), 1.0, 0.0)
         for t in range(CPD)
     ]
-    wanted_ref[...] = dot_nt(jnp.concatenate(leaf_rows, axis=0).astype(bf16), relation[...])
+    wanted_ref[...] = dot_nt(
+        jnp.concatenate(leaf_rows, axis=0).astype(bf16), relation[...]
+    ).astype(bf16)
 
     pick_row, pick_lane = iota((SHARE_PAD, WIDE), 0), iota((SHARE_PAD, WIDE), 1)
     pick16 = ((pick_lane == pick_row + SHARE * portion) & (pick_row < SHARE)).astype(f32).astype(bf16)
@@ -374,101 +410,25 @@
     line = jnp.sum(jnp.where(square, owner, 0.0), axis=0, keepdims=True)
     lists_ref[7:8, :] = line.astype(i32)
 
-    own.wait()
-    for copy in z_copies:
-        copy.wait()
-    y_copies = [
-        remote(gat_ref.at[row], gat_ref.at[row], y_send.at[k], y_recv.at[k], target)
-        for k, target in enumerate(y_targets)
-    ]
-    for copy in y_copies:
-        copy.start()
-    c_copies = []
-    for k in range(4):
-        at = core * 4 + lax.rem(y - k + 4, 4)
-        if k:
-            y_copies[k - 1].wait_recv()
-        copy = remote(gat_ref.at[at], gat_ref.at[at], c_send.at[k], c_recv.at[k], c_target)
-        copy.start()
-        c_copies.append(copy)
-    for copy in y_copies:
-        copy.wait_send()
-    for copy in c_copies:
-        copy.wait()
-
-
-def first(displacement, leaf_row, near_list, stiffness, surf, up_inverse):
-    npoints = displacement.shape[1]
-    sides = len(OFFSETS)
-    dma = pltpu.SemaphoreType.DMA
-    return pl.pallas_call(
-        first_kernel,
-        out_shape=(
-            jax.ShapeDtypeStruct((10, 48, WIDE), f32),
-            jax.ShapeDtypeStruct((8, 128), i32),
-            jax.ShapeDtypeStruct((8, 8, 16, 128), f32),
-            jax.ShapeDtypeStruct((8 * CPD, 160), f32),
-            jax.ShapeDtypeStruct((3 * CPD, SHARE_PAD, DEPTH), bf16),
-            jax.ShapeDtypeStruct((CPD, 3, SHARE_PAD, 128), f32),
-        ),
-        in_specs=[VMEM] * 6,
-        out_specs=(VMEM,) * 6,
-        scratch_shapes=[
-            pltpu.VMEM((sides, 3, npoints), f32),
-            pltpu.VMEM((sides, 1, npoints), i32),
-            pltpu.VMEM((144, WIDE), f32),
-            pltpu.VMEM((48, WIDE), i32),
-            pltpu.VMEM((144, NPT), f32),
-            pltpu.VMEM((FAR, 128), i32),
-            pltpu.VMEM((160, 128), bf16),
-            pltpu.VMEM((3, EQUIV, 128), f32),
-            pltpu.VMEM((ROWS, CPD * WIDE), bf16),
-            pltpu.VMEM((ROWS, CPD * WIDE), bf16),
-            pltpu.VMEM((PER_OWNER, CPD * WIDE), bf16),
-            pltpu.VMEM((ROWS, PER_OWNER), f32),
-            pltpu.VMEM((ROWS, PER_OWNER), f32),
-            pltpu.VMEM((16, 128), f32),
-            dma((sides,)),
-            dma((sides,)),
-            dma((sides,)),
-            dma((sides,)),
-            dma,
-            dma((7,)),
-            dma((7,)),
-            dma((3,)),
-            dma((3,)),
-            dma((4,)),
-            dma((4,)),
-        ],
-        compiler_params=pltpu.CompilerParams(collective_id=0, has_side_effects=True),
-        name="first",
-    )(displacement, leaf_row, near_list, stiffness, surf, up_inverse)
-
-
-def near_kernel(
-    lists, comp_ref, wanted_ref, lefts, spots, out_ref, rights, even_pairs, odd_pairs, sums
-):
-    portion = lax.axis_index("leaf")
-    wanted = wanted_ref[...].astype(bf16)
     feature = iota((FEATURES, WIDE), 0)
     turn = lax.rem(feature, 6)
-    first = (feature < 18) & ((turn == 0) | (turn == 3) | (turn == 5)) | (feature == 21)
-    second = (feature < 18) & ((turn == 1) | (turn == 4)) | (feature == 22)
+    use_top = (feature < 18) & ((turn == 0) | (turn == 3) | (turn == 5)) | (feature == 21)
+    use_middle = (feature < 18) & ((turn == 1) | (turn == 4)) | (feature == 22)
 
     def factors(x, y, z, last):
         value = jnp.where(
             feature < 6, x, jnp.where(feature < 12, y, jnp.where(feature < 18, z, last))
         )
         top, middle, low = thirds(value)
-        return jnp.where(first, top, jnp.where(second, middle, low))
+        return jnp.where(use_top, top, jnp.where(use_middle, middle, low))
 
     def some_sources(index, carry):
-        cells = [lists[6, BATCH * index + k] for k in range(BATCH)]
+        cells = [BATCH * index + k for k in range(BATCH)]
         rels = [comp_ref[REL, pl.ds(c, 1), :].astype(i32) for c in cells]
         hits = [
             (iota((160, WIDE), 0) == rel - 2 * PER_OWNER).astype(f32).astype(bf16) for rel in rels
         ]
-        reaches = [dot(wanted, hit) for hit in hits]
+        reaches = [dot(wanted_ref[...], hit) for hit in hits]
         for k, c in enumerate(cells):
             rel = rels[k]
             px = comp_ref[PX, pl.ds(c, 1), :] - (4 * (rel >> 5) + 2).astype(f32)
@@ -482,13 +442,108 @@
             push_rows = factors(fx, fy, fz, -along)
             push_rows = jnp.where((feature >= 18) & (feature < 21), 0.0, push_rows)
             mask_rows = FAR_AWAY - FAR_AWAY * reaches[k]
-            rights[c, :, 0:WIDE] = jnp.concatenate([near_rows, mask_rows], axis=0).astype(bf16)
-            rights[c, 0:FEATURES, WIDE : 2 * WIDE] = push_rows.astype(bf16)
-            rights[c, FEATURES:DEPTH, WIDE : 2 * WIDE] = jnp.zeros((8 * CPD, WIDE), bf16)
+            rights_ref[c, :, 0:WIDE] = jnp.concatenate([near_rows, mask_rows], axis=0).astype(bf16)
+            rights_ref[c, :, WIDE : 2 * WIDE] = jnp.concatenate(
+                [push_rows, jnp.zeros((8 * CPD, WIDE), f32)], axis=0
+            ).astype(bf16)
         return carry
 
-    lax.fori_loop(0, (lists[6, COUNT] + (BATCH - 1)) // BATCH, some_sources, 0)
-    rights[DUMMY] = jnp.where(iota((DEPTH, 2 * WIDE), 0) == 21, FAR_AWAY, 0.0).astype(bf16)
+    rights_ref[DUMMY] = jnp.where(iota((DEPTH, 2 * WIDE), 0) == 21, FAR_AWAY, 0.0).astype(bf16)
+    lax.fori_loop(0, EARLY, some_sources, 0)
+
+    own.wait()
+    y_copies, c_copies = [], []
+
+    def pass_on(at, where, index):
+        place = gat_ref.at[at, where]
+        copy = remote(place, place, c_send.at[index], c_recv.at[index], c_target)
+        copy.start()
+        c_copies.append(copy)
+
+    for order, k in enumerate((0, 1, 7, 2, 6, 3, 5, 4)):
+        where = lax.rem(z - k + 8, 8)
+        if k:
+            z_copies[k - 1].wait_recv()
+        place = gat_ref.at[row, where]
+        for side, target in enumerate(y_targets):
+            index = 3 * order + side
+            copy = remote(place, place, y_send.at[index], y_recv.at[index], target)
+            copy.start()
+            y_copies.append(copy)
+        pass_on(row, where, order)
+    lax.fori_loop(EARLY, CELLS // BATCH, some_sources, 0)
+    for order, k in enumerate((0, 1, 7, 2, 6, 3, 5, 4)):
+        where = lax.rem(z - k + 8, 8)
+        for side in range(3):
+            index = 3 * order + side
+            y_copies[index].wait_recv()
+            pass_on(core * 4 + lax.rem(y - side + 3, 4), where, 8 + index)
+    for copy in (*z_copies, *y_copies):
+        copy.wait_send()
+    for copy in c_copies:
+        copy.wait()
+
+
+def first(displacement, point_leaf, near_list, stiffness, surf, up_inverse):
+    npoints = displacement.shape[1]
+    sides = len(OFFSETS)
+    dma = pltpu.SemaphoreType.DMA
+    return pl.pallas_call(
+        first_kernel,
+        out_shape=(
+            jax.ShapeDtypeStruct((10, 48, WIDE), f32),
+            jax.ShapeDtypeStruct((8, 128), i32),
+            jax.ShapeDtypeStruct((8, 8, 16, 128), f32),
+            jax.ShapeDtypeStruct((3 * CPD, SHARE_PAD, DEPTH), bf16),
+            jax.ShapeDtypeStruct((CPD, 3, SHARE_PAD, 128), f32),
+            jax.ShapeDtypeStruct((CELLS + 1, DEPTH, 2 * WIDE), bf16),
+        ),
+        in_specs=[HBM] * 6,
+        out_specs=(VMEM,) * 6,
+        scratch_shapes=[
+            pltpu.VMEM((sides, 3, npoints), f32),
+            pltpu.VMEM((sides, 1, npoints), i32),
+            pltpu.VMEM((3, npoints), f32),
+            pltpu.VMEM((EQUIV, 8), f32),
+            pltpu.VMEM((1, npoints), i32),
+            pltpu.VMEM((2, FAR, 128), i32),
+            pltpu.VMEM((NPT, NPT), f32),
+            pltpu.VMEM((ROWS, ROWS), f32),
+            pltpu.VMEM((144, WIDE), f32),
+            pltpu.VMEM((48, WIDE), i32),
+            pltpu.VMEM((144, NPT), f32),
+            pltpu.VMEM((FAR, 128), i32),
+            pltpu.VMEM((160, 128), bf16),
+            pltpu.VMEM((8 * CPD, 160), bf16),
+            pltpu.VMEM((3, EQUIV, 128), f32),
+            pltpu.VMEM((ROWS, CPD * WIDE), bf16),
+            pltpu.VMEM((ROWS, CPD * WIDE), bf16),
+            pltpu.VMEM((PER_OWNER, CPD * WIDE), bf16),
+            pltpu.VMEM((ROWS, PER_OWNER), f32),
+            pltpu.VMEM((ROWS, PER_OWNER), f32),
+            pltpu.VMEM((16, 128), f32),
+            dma((sides,)),
+            dma((sides,)),
+            dma((sides,)),
+            dma((sides,)),
+            dma((7,)),
+            dma,
+            dma((7,)),
+            dma((7,)),
+            dma((24,)),
+            dma((24,)),
+            dma((32,)),
+            dma((32,)),
+        ],
+        compiler_params=pltpu.CompilerParams(
+            collective_id=0, has_side_effects=True, vmem_limit_bytes=LIMIT
+        ),
+        name="first",
+    )(*(in_hbm(x) for x in (displacement, point_leaf, near_list, stiffness, surf, up_inverse)))
+
+
+def near_kernel(lists, comp_ref, lefts, spots, rights, out_ref, even_pairs, odd_pairs, sums):
+    portion = lax.axis_index("leaf")
 
     def multiply(t, index, products):
         c = lists[t, index]
@@ -517,51 +572,60 @@
                 else:
                     added = [u + v for u, v in zip(added, part)]
             for a in range(4):
-                sums[a, at, :] += added[a]
-
-    pick_row, pick_lane = iota((SHARE_PAD, WIDE), 0), iota((SHARE_PAD, WIDE), 1)
-    pick = (pick_lane == pick_row + SHARE * portion) & (pick_row < SHARE)
+                sums[t, a, at, :] += added[a]
+
+    sums[...] = jnp.zeros_like(sums)
+    multiply(0, 0, even_pairs)
 
     def one_target(t, carry):
-        sums[...] = jnp.zeros_like(sums)
-        multiply(t, 0, even_pairs)
+        steps = (lists[t, COUNT] + 1) // 2
 
         def two_pairs(index, carry):
             multiply(t, 2 * index + 1, odd_pairs)
             add_pair(t, 2 * index, even_pairs)
-            multiply(t, 2 * index + 2, even_pairs)
+            ends = index + 1 == steps
+            after = jnp.where(ends, jnp.minimum(t + 1, CPD - 1), t)
+            multiply(after, jnp.where(ends, 0, 2 * index + 2), even_pairs)
             add_pair(t, 2 * index + 1, odd_pairs)
             return carry
 
-        lax.fori_loop(0, (lists[t, COUNT] + 1) // 2, two_pairs, 0)
-        for a in range(3):
-            total = sums[a] + spots[t, a] * sums[3]
-            column = jnp.sum(total, axis=1, keepdims=True) * inv_eight_pi
-            row = jnp.sum(jnp.where(pick, column, 0.0), axis=0, keepdims=True)
-            out_ref[a, pl.ds(t, 1), :] = row
+        lax.fori_loop(0, steps, two_pairs, 0)
         return carry
 
     lax.fori_loop(0, CPD, one_target, 0)
-
-
-def near_field(lists, comp, wanted, lefts, spots):
+    pick_row, pick_lane = iota((SHARE_PAD, WIDE), 0), iota((SHARE_PAD, WIDE), 1)
+    pick = (pick_lane == pick_row + SHARE * portion) & (pick_row < SHARE)
+
+    def finish(index, carry):
+        for t in (2 * index, 2 * index + 1):
+            for a in range(3):
+                total = sums[t, a] + spots[t, a] * sums[t, 3]
+                column = jnp.sum(total, axis=1, keepdims=True) * inv_eight_pi
+                row = jnp.sum(jnp.where(pick, column, 0.0), axis=0, keepdims=True)
+                out_ref[a, pl.ds(t, 1), :] = row
+        return carry
+
+    lax.fori_loop(0, CPD // 2, finish, 0)
+
+
+def near_field(lists, comp, lefts, spots, rights):
     return pl.pallas_call(
         near_kernel,
         out_shape=jax.ShapeDtypeStruct((3, 8, WIDE), f32),
         in_specs=[SMEM] + [VMEM] * 4,
         out_specs=VMEM,
         scratch_shapes=[
-            pltpu.VMEM((CELLS + 1, DEPTH, 2 * WIDE), bf16),
             pltpu.VMEM((SHARE_PAD, 2 * WIDE), f32),
             pltpu.VMEM((SHARE_PAD, 2 * WIDE), f32),
-            pltpu.VMEM((4, SHARE_PAD, 128), f32),
+            pltpu.VMEM((CPD, 4, SHARE_PAD, 128), f32),
         ],
+        compiler_params=pltpu.CompilerParams(vmem_limit_bytes=LIMIT),
         name="near_field",
-    )(lists, comp, wanted, lefts, spots)
+    )(lists, comp, lefts, spots, rights)
 
 
 def far_part(
-    points, gat_ref, far_ref, surf_ref, inverse_ref, local_ref, far4, sources, packed, pushes, mids, total
+    points, gat_ref, far_ref, far_load, surf_ref, inverse_ref, local_ref, far4, sources, packed, pushes, mids, total
 ):
     me = lax.axis_index("cells")
     portion = lax.axis_index("leaf")
@@ -584,8 +648,8 @@
 
     lax.fori_loop(0, 8, one_tile, 0)
 
-    block = pl.multiple_of(me // 4 * 128, 128)
-    entries = far_ref[:, pl.ds(block, 128)]
+    far_load.wait()
+    entries = far_ref[...]
     mine = lax.rem(me, 4)
     lane48 = iota((FAR, 128), 1) // PER_OWNER
     picked = jnp.zeros((FAR, 128), i32)
@@ -651,12 +715,14 @@
 def last_kernel(
     points,
     gat_ref,
-    far_ref,
+    far_hbm,
     surf_ref,
     inverse_ref,
     comp_ref,
     near_ref,
     out_ref,
+    far_ref,
+    load_sem,
     far4,
     sources,
     packed,
@@ -674,13 +740,16 @@
     send_part,
     recv_part,
 ):
+    block = pl.multiple_of(lax.axis_index("cells") // 4 * 128, 128)
+    far_load = pltpu.make_async_copy(far_hbm.at[:, pl.ds(block, 128)], far_ref, load_sem)
+    far_load.start()
     sides = beside("cells", (1, -1))
     mates = beside("leaf", (1, 2, 3))
     barrier = pltpu.get_barrier_semaphore()
     for target in (*sides, *mates):
         pl.semaphore_signal(barrier, inc=1, device_id=target, device_id_type=MESH)
     far_part(
-        points, gat_ref, far_ref, surf_ref, inverse_ref, local_ref, far4, sources, packed, pushes, mids, total
+        points, gat_ref, far_ref, far_load, surf_ref, inverse_ref, local_ref, far4, sources, packed, pushes, mids, total
     )
     pl.semaphore_wait(barrier, 5)
     copies = [
@@ -735,9 +804,11 @@
     return pl.pallas_call(
         last_kernel,
         out_shape=jax.ShapeDtypeStruct((3, npoints), f32),
-        in_specs=[SMEM] + [VMEM] * 6,
+        in_specs=[SMEM, VMEM, HBM] + [VMEM] * 4,
         out_specs=VMEM,
         scratch_shapes=[
+            pltpu.VMEM((FAR, 128), i32),
+            dma,
             pltpu.VMEM((4, FAR, 128), i32),
             pltpu.VMEM((16, 128), i32),
             pltpu.VMEM((8, 96, 256), bf16),
@@ -755,19 +826,21 @@
             dma((3,)),
             dma((3,)),
         ],
-        compiler_params=pltpu.CompilerParams(collective_id=1, has_side_effects=True),
+        compiler_params=pltpu.CompilerParams(
+            collective_id=1, has_side_effects=True, vmem_limit_bytes=LIMIT
+        ),
         name="last",
-    )(points, gathered, far_list, surf, down_inverse, comp, near)
+    )(points, gathered, in_hbm(far_list), surf, down_inverse, comp, near)
 
 
 def body(displacement, point_leaf, near_list, far_list, stiffness, up_inverse, down_inverse):
     table = surface_table()
     surf = jnp.asarray(np.pad(table, ((0, 0), (0, 5))))
     points = jnp.asarray((inner_radius * table).astype(np.float32).reshape(-1))
-    comp, lists, gathered, wanted, lefts, spots = first(
-        displacement, point_leaf[None, :], near_list, stiffness, surf, up_inverse
+    comp, lists, gathered, lefts, spots, rights = first(
+        displacement, point_leaf, near_list, stiffness, surf, up_inverse
     )
-    near = near_field(lists, comp, wanted, lefts, spots)
+    near = near_field(lists, comp, lefts, spots, rights)
     return last(
         points, gathered, far_list, surf, down_inverse, comp, near, displacement.shape[1]
     )

time: 74.8 us -> 63.2 us (0.84)
  the two profiles are of different devices: /device:TPU:8 before, /device:TPU:1 now
where the time goes in v2:
time: 63.2 us; the launch traced here: 63.5 us
  Pallas kernels  62.8 us (99%)
    pallas_call x1, Pallas kernels, first(): pl.pallas_call(first_kernel, out_shape=(jax.ShapeDtypeStruct((10, 48, WID...  30.7 us
    pallas_call x1, Pallas kernels, last(): pl.pallas_call(last_kernel, out_shape=jax.ShapeDtypeStruct((3, npoints),...  21.6 us
    pallas_call x1, Pallas kernels, near_field(): pl.pallas_call(near_kernel, out_shape=jax.ShapeDtypeStruct((3, 8, WIDE),...  10.5 us

profile of v2, /device:TPU:1, one launch (start us, length us, event | category | flops | bytes accessed | tf_op | source)
XLA Modules:
  0.0 63.5 jit_solution(2804967535082593593)
XLA Ops:
  0.0 0.0 copy-start.1
  0.0 0.0 copy-start.2
  0.0 0.0 copy-start
  0.0 30.7 %first.1 = (f32[10,48,384]{2,1,0:T(8,128)S(1)}, s32[8,128]{1,0:T(8,128)S(1)}, f32[8,8,16,128]{3,2,1,0:T(8,128)S(1)}, bf16[18,80,72]{2,1,0:T(8,128)(2,1)S(1)}, f3...) custom-call(f32[3,1872]{1,0:T(4,128)} %disp_hbm.1, s32[1872]{0:T(1024)} %leaf_hbm.1, s32[48,2048]{1,0:T(8,128)} %near_hbm.1, ...), custom_call_target="tpu_custom_call" | custom-call | tf_op jit(solution)/shard_map/first/pallas_call | solution.py:491
  30.7 10.5 %near_field.1.near_ref = f32[3,8,384]{2,1,0:T(8,128)S(1)} custom-call(s32[8,128]{1,0:T(8,128)S(1)} %get-tuple-element.13.lists, f32[10,48,384]{2,1,0:T(8,128)S(1)} %get-tuple-element.12.comp_ref, bf16[18,80,72]{2,1,0:T(8,128)(2,1)S(1)} %get-tuple-element.14.lefts, f32[6,3,80,128]{3,2,1,0:T(8,128)S(1)} %get-tuple-element.15.spots, ...), custom_call_target="tpu_custom_call" | custom-call | tf_op jit(solution)/shard_map/near_field/pallas_call | solution.py:612
  41.2 0.0 copy-done.1
  41.2 0.0 copy-done.2
  41.2 0.0 copy-done
  41.2 21.6 %last.1 = f32[3,1872]{1,0:T(4,128)S(1)} custom-call(f32[168]{0:T(256)S(1)} %copy-done.2, f32[8,8,16,128]{3,2,1,0:T(8,128)S(1)} %get-tuple-element.11.gat_ref, s32[48,2048]{1,0:T(8,128)} %far_hbm.1, f32[56,8]{1,0:T(8,128)S(1)} %copy-done.1, f32[168,168]{1,0:T(8,128)S(1)} %copy-done, f32[10,48,384]{2,1,0:T(8,128)S(1)} %get-tuple-element.12.comp_ref, ...), custom_call_target="tpu_custom_call" | custom-call | tf_op jit(solution)/shard_map/last/pallas_call | solution.py:804
  62.8 0.6 copy.11
Async XLA Ops:
  0.0 41.2 %copy-start.1 = (f32[56,8]{1,0:T(8,128)S(1)}, f32[56,8]{1,0:T(8,128)}, u32[]{:S(2)}) copy-start(f32[56,8]{1,0:T(8,128)} %constant.4.clone.surf_hbm.surf_ref) | copy-start | bytes 5380
  0.0 41.2 %copy-start.2 = (f32[168]{0:T(256)S(1)}, f32[168]{0:T(256)}, u32[]{:S(2)}) copy-start(f32[168]{0:T(256)} %constant.5.clone.points) | copy-start | bytes 2020
  0.0 41.2 %copy-start = (f32[168,168]{1,0:T(8,128)S(1)}, f32[168,168]{1,0:T(8,128)}, u32[]{:S(2)}) copy-start(f32[168,168]{1,0:T(8,128)} %inverse_ref.1) | copy-start | bytes 338692

commit v3 on v2

--- a/solution.py
+++ b/solution.py
@@ -77,8 +77,10 @@
 LIMIT = 20 << 20
 HBM = pl.BlockSpec(memory_space=pltpu.HBM)
 DUMMY = CELLS
-BATCH = 3
-EARLY = 7
+BATCH = 6
+PARTS = 2
+EARLY = 5
+MIDDLE = 3
 
 
 def thirds(value):
@@ -124,6 +126,32 @@
     count = lax.axis_size(axis)
     me = lax.axis_index(axis)
     return [{axis: lax.rem(me + (off + count), count)} for off in offsets]
+
+
+def add_pair(comp_ref, sums, t, c, products):
+    p = [comp_ref[PX + a, pl.ds(c, 1), :] for a in range(3)]
+    f = [comp_ref[FX + a, pl.ds(c, 1), :] for a in range(3)]
+    for part in range(PARTS):
+        groups = range(part * 10 // PARTS, (part + 1) * 10 // PARTS)
+        added = {}
+        for b in range(WIDE // 128):
+            lanes = slice(128 * b, 128 * b + 128)
+            pb = [value[:, lanes] for value in p]
+            fb = [value[:, lanes] for value in f]
+            for g in groups:
+                at = slice(8 * g, 8 * g + 8)
+                shifted = products[at, lanes]
+                inner = products[at, WIDE + 128 * b : WIDE + 128 * b + 128]
+                root = lax.rsqrt(shifted)
+                cube = root * root * root
+                even = root + smooth_sq * cube
+                along = cube * inner
+                one = [even * fb[a] - along * pb[a] for a in range(3)] + [along]
+                added[g] = [u + v for u, v in zip(added[g], one)] if b else one
+        for g in groups:
+            at = slice(8 * g, 8 * g + 8)
+            for a in range(4):
+                sums[t, a, at, :] += added[g][a]
 
 
 def first_kernel(
@@ -139,6 +167,7 @@
     lefts_ref,
     spots_ref,
     rights_ref,
+    sums_ref,
     held_disp,
     held_leaf,
     disp_ref,
@@ -154,12 +183,16 @@
     relation,
     wanted_ref,
     wide,
+    owned_ref,
     terms_top,
     terms_low,
     member_ref,
     total,
     density,
     block_ref,
+    even_pairs,
+    odd_pairs,
+    owners_ref,
     send_disp,
     recv_disp,
     send_leaf,
@@ -331,14 +364,27 @@
     for a in range(3):
         comp_ref[FX + a, 0:48, 0:NPT] = force[48 * a : 48 * a + 48, :]
 
+    cell = iota((48, 1), 0)
+    mine = (jnp.floor(first * (1.0 / PER_OWNER)) == 4.0) & (cell < OWNABLE)
+    mine = jnp.where(mine, 1.0, 0.0)
+    before = (iota((48, 48), 0) > iota((48, 48), 1)).astype(f32)
+    rank = dot(before, jnp.broadcast_to(mine, (48, 128)))
+    chosen = jnp.where((rank == iota((48, 128), 1).astype(f32)) & (mine > 0.0), 1.0, 0.0)
+    chosen = jnp.concatenate([chosen] * 3, axis=0).astype(bf16)
+    for k, part in enumerate((DX, DY, DZ, FX, FY, FZ, REL)):
+        pieces = jnp.concatenate(thirds(comp_ref[part]), axis=0).astype(bf16)
+        found = lax.dot_general(
+            chosen, pieces, (((0,), (0,)), ((), ())), preferred_element_type=f32
+        )
+        owned_ref[k] = found[0:16]
     total[...] = jnp.zeros_like(total)
 
     def one_home(home, carry):
-        for k in range(CPD):
-            c = CPD * home + k
-            d = [comp_ref[DX + a, pl.ds(c, 1), :] for a in range(3)]
-            f = [comp_ref[FX + a, pl.ds(c, 1), :] for a in range(3)]
-            rel = comp_ref[REL, pl.ds(c, 1), :].astype(i32) - 4 * PER_OWNER
+        for k in range(3):
+            c = 3 * home + k
+            d = [owned_ref[a, pl.ds(c, 1), :] for a in range(3)]
+            f = [owned_ref[3 + a, pl.ds(c, 1), :] for a in range(3)]
+            rel = owned_ref[6, pl.ds(c, 1), :].astype(i32) - 4 * PER_OWNER
             member = (iota((PER_OWNER, WIDE), 0) == rel).astype(f32).astype(bf16)
             member_ref[:, WIDE * k : WIDE * (k + 1)] = member
             for b in range(WIDE // 128):
@@ -382,20 +428,15 @@
     high = jnp.floor(last * (1.0 / 16.0))
     lane = iota((48, 128), 1)
     which = iota((48, 1), 0).astype(f32)
-    real = which < float(CELLS)
+    real = (which < float(CELLS)) & (which >= float(CPD))
     flags = []
     for t in range(CPD):
         low_t, high_t = low[t : t + 1], high[t : t + 1]
         flags.append(jnp.where((high >= low_t - 1.0) & (low <= high_t + 1.0) & real, 1.0, 0.0))
     owner = jnp.floor(low * 0.5)
-    union = flags[0]
-    for t in range(1, CPD):
-        union = jnp.maximum(union, flags[t])
-    flags.append(union)
     table = jnp.zeros((48, 128), f32)
     for t, flag in enumerate(flags):
         table = table + jnp.where(lane == t, flag, 0.0)
-    before = (iota((48, 48), 0) > iota((48, 48), 1)).astype(f32)
     rank = dot(before, table)
     count = jnp.sum(table, axis=0, keepdims=True)
     lane_row = iota((1, 128), 1)
@@ -448,6 +489,26 @@
             ).astype(bf16)
         return carry
 
+    owners_ref[...] = jnp.broadcast_to(owner[0:8], (8, 128))
+
+    def multiply_own(t, c, products):
+        apart = owners_ref[pl.ds(c, 1), 0:1] - owners_ref[pl.ds(t, 1), 0:1]
+        left = [lefts_ref[3 * t + w].astype(f32) for w in range(3)]
+        left = jnp.where(apart < -0.5, left[0], jnp.where(apart > 0.5, left[2], left[1]))
+        products[...] = dot(left.astype(bf16), rights_ref[c])
+
+    def own_target(t, carry):
+        for k in range(CPD // 2):
+            multiply_own(t, 2 * k + 1, odd_pairs)
+            add_pair(comp_ref, sums_ref, t, 2 * k, even_pairs)
+            if k + 1 < CPD // 2:
+                multiply_own(t, 2 * k + 2, even_pairs)
+            else:
+                multiply_own(jnp.minimum(t + 1, CPD - 1), 0, even_pairs)
+            add_pair(comp_ref, sums_ref, t, 2 * k + 1, odd_pairs)
+        return carry
+
+    sums_ref[...] = jnp.zeros_like(sums_ref)
     rights_ref[DUMMY] = jnp.where(iota((DEPTH, 2 * WIDE), 0) == 21, FAR_AWAY, 0.0).astype(bf16)
     lax.fori_loop(0, EARLY, some_sources, 0)
 
@@ -472,12 +533,15 @@
             y_copies.append(copy)
         pass_on(row, where, order)
     lax.fori_loop(EARLY, CELLS // BATCH, some_sources, 0)
+    multiply_own(0, 0, even_pairs)
+    lax.fori_loop(0, MIDDLE, own_target, 0)
     for order, k in enumerate((0, 1, 7, 2, 6, 3, 5, 4)):
         where = lax.rem(z - k + 8, 8)
         for side in range(3):
             index = 3 * order + side
             y_copies[index].wait_recv()
             pass_on(core * 4 + lax.rem(y - side + 3, 4), where, 8 + index)
+    lax.fori_loop(MIDDLE, CPD, own_target, 0)
     for copy in (*z_copies, *y_copies):
         copy.wait_send()
     for copy in c_copies:
@@ -497,9 +561,10 @@
             jax.ShapeDtypeStruct((3 * CPD, SHARE_PAD, DEPTH), bf16),
             jax.ShapeDtypeStruct((CPD, 3, SHARE_PAD, 128), f32),
             jax.ShapeDtypeStruct((CELLS + 1, DEPTH, 2 * WIDE), bf16),
+            jax.ShapeDtypeStruct((CPD, 4, SHARE_PAD, 128), f32),
         ),
         in_specs=[HBM] * 6,
-        out_specs=(VMEM,) * 6,
+        out_specs=(VMEM,) * 7,
         scratch_shapes=[
             pltpu.VMEM((sides, 3, npoints), f32),
             pltpu.VMEM((sides, 1, npoints), i32),
@@ -516,12 +581,16 @@
             pltpu.VMEM((160, 128), bf16),
             pltpu.VMEM((8 * CPD, 160), bf16),
             pltpu.VMEM((3, EQUIV, 128), f32),
-            pltpu.VMEM((ROWS, CPD * WIDE), bf16),
-            pltpu.VMEM((ROWS, CPD * WIDE), bf16),
-            pltpu.VMEM((PER_OWNER, CPD * WIDE), bf16),
+            pltpu.VMEM((7, 16, WIDE), f32),
+            pltpu.VMEM((ROWS, 3 * WIDE), bf16),
+            pltpu.VMEM((ROWS, 3 * WIDE), bf16),
+            pltpu.VMEM((PER_OWNER, 3 * WIDE), bf16),
             pltpu.VMEM((ROWS, PER_OWNER), f32),
             pltpu.VMEM((ROWS, PER_OWNER), f32),
             pltpu.VMEM((16, 128), f32),
+            pltpu.VMEM((SHARE_PAD, 2 * WIDE), f32),
+            pltpu.VMEM((SHARE_PAD, 2 * WIDE), f32),
+            pltpu.VMEM((8, 128), f32),
             dma((sides,)),
             dma((sides,)),
             dma((sides,)),
@@ -542,7 +611,7 @@
     )(*(in_hbm(x) for x in (displacement, point_leaf, near_list, stiffness, surf, up_inverse)))
 
 
-def near_kernel(lists, comp_ref, lefts, spots, rights, out_ref, even_pairs, odd_pairs, sums):
+def near_kernel(lists, comp_ref, lefts, spots, rights, own_sums, out_ref, even_pairs, odd_pairs, sums):
     portion = lax.axis_index("leaf")
 
     def multiply(t, index, products):
@@ -550,43 +619,19 @@
         w = jnp.clip(lists[7, c] - lists[7, t] + 1, 0, 2)
         products[...] = dot(lefts[3 * t + w], rights[c])
 
-    def add_pair(t, index, products):
-        c = lists[t, index]
-        p = [comp_ref[PX + a, pl.ds(c, 1), :] for a in range(3)]
-        f = [comp_ref[FX + a, pl.ds(c, 1), :] for a in range(3)]
-        for g in range(SHARE_PAD // 8):
-            at = slice(8 * g, 8 * g + 8)
-            added = None
-            for b in range(WIDE // 128):
-                lanes = slice(128 * b, 128 * b + 128)
-                shifted = products[at, lanes]
-                inner = products[at, WIDE + 128 * b : WIDE + 128 * b + 128]
-                root = lax.rsqrt(shifted)
-                cube = root * root * root
-                even = root + smooth_sq * cube
-                along = cube * inner
-                part = [even * f[a][:, lanes] - along * p[a][:, lanes] for a in range(3)]
-                part.append(along)
-                if added is None:
-                    added = part
-                else:
-                    added = [u + v for u, v in zip(added, part)]
-            for a in range(4):
-                sums[t, a, at, :] += added[a]
-
-    sums[...] = jnp.zeros_like(sums)
+    sums[...] = own_sums[...]
     multiply(0, 0, even_pairs)
 
     def one_target(t, carry):
-        steps = (lists[t, COUNT] + 1) // 2
+        steps = jnp.maximum((lists[t, COUNT] + 1) // 2, 1)
 
         def two_pairs(index, carry):
             multiply(t, 2 * index + 1, odd_pairs)
-            add_pair(t, 2 * index, even_pairs)
+            add_pair(comp_ref, sums, t, lists[t, 2 * index], even_pairs)
             ends = index + 1 == steps
             after = jnp.where(ends, jnp.minimum(t + 1, CPD - 1), t)
             multiply(after, jnp.where(ends, 0, 2 * index + 2), even_pairs)
-            add_pair(t, 2 * index + 1, odd_pairs)
+            add_pair(comp_ref, sums, t, lists[t, 2 * index + 1], odd_pairs)
             return carry
 
         lax.fori_loop(0, steps, two_pairs, 0)
@@ -608,11 +653,11 @@
     lax.fori_loop(0, CPD // 2, finish, 0)
 
 
-def near_field(lists, comp, lefts, spots, rights):
+def near_field(lists, comp, lefts, spots, rights, own_sums):
     return pl.pallas_call(
         near_kernel,
         out_shape=jax.ShapeDtypeStruct((3, 8, WIDE), f32),
-        in_specs=[SMEM] + [VMEM] * 4,
+        in_specs=[SMEM] + [VMEM] * 5,
         out_specs=VMEM,
         scratch_shapes=[
             pltpu.VMEM((SHARE_PAD, 2 * WIDE), f32),
@@ -621,11 +666,30 @@
         ],
         compiler_params=pltpu.CompilerParams(vmem_limit_bytes=LIMIT),
         name="near_field",
-    )(lists, comp, lefts, spots, rights)
+    )(lists, comp, lefts, spots, rights, own_sums)
 
 
 def far_part(
-    points, gat_ref, far_ref, far_load, surf_ref, inverse_ref, local_ref, far4, sources, packed, pushes, mids, total
+    left_ref,
+    quarter_ref,
+    points,
+    gat_ref,
+    far_ref,
+    far_load,
+    surf_ref,
+    inverse_ref,
+    local_ref,
+    far4,
+    sources,
+    packed,
+    pushes,
+    mids,
+    total,
+    quarter,
+    even_rows,
+    odd_rows,
+    even_blocks,
+    odd_blocks,
 ):
     me = lax.axis_index("cells")
     portion = lax.axis_index("leaf")
@@ -690,22 +754,71 @@
     lax.fori_loop(0, 6, one_gather, 0)
     total[...] = jnp.zeros_like(total)
 
-    def one_block(index, carry):
+    left = left_ref[...].astype(bf16)
+    for a in range(3):
+        quarter[a] = jnp.broadcast_to(quarter_ref[portion, :, a : a + 1], (16, 128))
+    steps = thirds(jnp.full((16, 128), (inner_radius / 3.0) ** 2, f32))
+    for rows in (even_rows, odd_rows):
+        rows[...] = jnp.zeros_like(rows)
+        for k in range(3):
+            rows[pl.ds(12 + k, 16, stride=32), :] = steps[k]
+
+    def prepare_block(index, rows, blocks):
+        push = [pushes[index, 16 * a : 16 * a + 16, :] for a in range(3)]
+        gap = [mids[a, pl.ds(index, 1), :] - quarter[a] for a in range(3)]
+        square = (gap[0] * gap[0] + gap[1] * gap[1]) + (gap[2] * gap[2] + smooth_sq)
+        inner = (gap[0] * push[0] + gap[1] * push[1]) + gap[2] * push[2]
+        scale = inner_radius / 3.0
+        for a in range(3):
+            for k, third in enumerate(thirds((2.0 * scale) * gap[a])):
+                rows[pl.ds(3 * a + k, 16, stride=32), :] = third
+            for k, third in enumerate(thirds(scale * push[a])):
+                rows[pl.ds(16 + 3 * a + k, 16, stride=32), :] = third
+        for k, third in enumerate(thirds(square)):
+            rows[pl.ds(9 + k, 16, stride=32), :] = third
+        for k, third in enumerate(thirds(inner)):
+            rows[pl.ds(25 + k, 16, stride=32), :] = third
+        for j in range(14):
+            right = jnp.concatenate(
+                [rows[32 * j : 32 * j + 16, :], rows[32 * j + 16 : 32 * j + 32, :]], axis=1
+            )
+            blocks[j] = dot(left, right.astype(bf16))
+
+    def add_block(index, blocks):
+        groups = EQUIV // 8
+        sums = [[jnp.zeros((8, 128), f32) for _ in range(4)] for _ in range(groups)]
+        for j in range(14):
+            f = [pushes[index, 16 * a + j : 16 * a + j + 1, :] for a in range(3)]
+            shift = [points[3 * (14 * portion + j) + a] for a in range(3)]
+            for g in range(groups):
+                at = slice(8 * g, 8 * g + 8)
+                shifted = blocks[j, at, 0:128]
+                inner = blocks[j, at, 128:256]
+                root = lax.rsqrt(shifted)
+                cube = root * root * root
+                even = root + smooth_sq * cube
+                along = cube * inner
+                for a in range(3):
+                    sums[g][a] = sums[g][a] + (even * f[a] - along * shift[a])
+                sums[g][3] = sums[g][3] + along
         mid = [mids[a, pl.ds(index, 1), :] for a in range(3)]
-        for g in range(EQUIV // 8):
+        for g in range(groups):
             at = slice(8 * g, 8 * g + 8)
-            check = [mid[a] + inner_radius * surf_ref[at, a : a + 1] for a in range(3)]
-            sums = [total[EQUIV * a + 8 * g : EQUIV * a + 8 * g + 8, :] for a in range(3)]
-            for j in range(14):
-                f = [pushes[index, 16 * a + j : 16 * a + j + 1, :] for a in range(3)]
-                r = [check[a] - points[3 * (14 * portion + j) + a] for a in range(3)]
-                even, along = pull(r, f)
-                sums = [sums[a] + (even * f[a] + along * r[a]) for a in range(3)]
             for a in range(3):
-                total[EQUIV * a + 8 * g : EQUIV * a + 8 * g + 8, :] = sums[a]
+                check = mid[a] + inner_radius * surf_ref[at, a : a + 1]
+                row = EQUIV * a + 8 * g
+                total[row : row + 8, :] += sums[g][a] + check * sums[g][3]
+
+    prepare_block(0, even_rows, even_blocks)
+
+    def two_blocks(index, carry):
+        prepare_block(2 * index + 1, odd_rows, odd_blocks)
+        add_block(2 * index, even_blocks)
+        prepare_block(jnp.minimum(2 * index + 2, 11), even_rows, even_blocks)
+        add_block(2 * index + 1, odd_blocks)
         return carry
 
-    lax.fori_loop(0, 12, one_block, 0)
+    lax.fori_loop(0, 6, two_blocks, 0)
     value = total[...] * inv_eight_pi
     value = value + pltpu.roll(value, 64, 1)
     value = value + pltpu.roll(value, 32, 1)
@@ -714,6 +827,8 @@
 
 def last_kernel(
     points,
+    left_ref,
+    quarter_ref,
     gat_ref,
     far_hbm,
     surf_ref,
@@ -729,10 +844,17 @@
     pushes,
     mids,
     total,
+    quarter,
+    even_rows,
+    odd_rows,
+    even_blocks,
+    odd_blocks,
     local_ref,
+    packed_local,
     held_local,
     factors,
     spread_ref,
+    cell_ref,
     part_ref,
     held_part,
     send_local,
@@ -743,41 +865,77 @@
     block = pl.multiple_of(lax.axis_index("cells") // 4 * 128, 128)
     far_load = pltpu.make_async_copy(far_hbm.at[:, pl.ds(block, 128)], far_ref, load_sem)
     far_load.start()
+    packed_local[...] = jnp.zeros_like(packed_local)
     sides = beside("cells", (1, -1))
     mates = beside("leaf", (1, 2, 3))
     barrier = pltpu.get_barrier_semaphore()
     for target in (*sides, *mates):
         pl.semaphore_signal(barrier, inc=1, device_id=target, device_id_type=MESH)
     far_part(
-        points, gat_ref, far_ref, far_load, surf_ref, inverse_ref, local_ref, far4, sources, packed, pushes, mids, total
+        left_ref,
+        quarter_ref,
+        points,
+        gat_ref,
+        far_ref,
+        far_load,
+        surf_ref,
+        inverse_ref,
+        local_ref,
+        far4,
+        sources,
+        packed,
+        pushes,
+        mids,
+        total,
+        quarter,
+        even_rows,
+        odd_rows,
+        even_blocks,
+        odd_blocks,
     )
     pl.semaphore_wait(barrier, 5)
+    lane = iota((48, 128), 1) // PER_OWNER
+    for k in range(4):
+        rows = min(48, ROWS - 48 * k)
+        piece = local_ref[48 * k : 48 * k + rows, :]
+        here = lane[0:rows] == k
+        packed_local[0:rows, :] = jnp.where(here, piece, packed_local[0:rows, :])
     copies = [
-        remote(local_ref, held_local.at[k], send_local.at[k], recv_local.at[k], target)
+        remote(packed_local, held_local.at[k], send_local.at[k], recv_local.at[k], target)
         for k, target in enumerate(sides)
     ]
     for copy in copies:
         copy.start()
     for copy in copies:
         copy.wait()
-    lane = iota((ROWS, 128), 1) // PER_OWNER
-    value = jnp.where(
-        lane == 0, held_local[0], jnp.where(lane == 1, local_ref[...], held_local[1])
-    )
-    top, low = halves(value)
-    factors[0:ROWS, :] = top
-    factors[ROWS : 2 * ROWS, :] = low
-
-    def one_cell(t, carry):
+    lane = iota((48, 128), 1) // PER_OWNER
+    for k in range(4):
+        rows = min(48, ROWS - 48 * k)
+        value = local_ref[48 * k : 48 * k + rows, :]
+        for side in range(2):
+            place = 2 * side
+            moved = held_local[side, 0:rows, :]
+            if place != k:
+                moved = pltpu.roll(moved, (PER_OWNER * (place - k)) % 128, 1)
+            value = jnp.where(lane[0:rows] == place, moved, value)
+        top, low = halves(value)
+        factors[48 * k : 48 * k + rows, 0:128] = top
+        factors[48 * k : 48 * k + rows, 128:256] = low
+
+    def spread_out(t):
         rel = comp_ref[REL, pl.ds(t, 1), :].astype(i32) - 3 * PER_OWNER
         member = (iota((128, WIDE), 0) == rel).astype(f32).astype(bf16)
-        both = dot(factors[...], member)
-        spread_ref[t] = both[0:ROWS] + both[ROWS : 2 * ROWS]
+        spread_ref[t] = dot(factors[...], jnp.concatenate([member, member], axis=0))
+
+    def three_cells(index, carry):
+        for k in range(3):
+            spread_out(3 * index + k)
         return carry
 
-    lax.fori_loop(0, CPD, one_cell, 0)
-    for t in range(CPD):
-        d = [comp_ref[DX + a, t : t + 1, :] for a in range(3)]
+    lax.fori_loop(0, 2, three_cells, 0)
+
+    def one_cell(t, carry):
+        d = [comp_ref[DX + a, pl.ds(t, 1), :] for a in range(3)]
         sums = [jnp.zeros((8, WIDE), f32) for _ in range(3)]
         for g in range(EQUIV // 8):
             at = slice(8 * g, 8 * g + 8)
@@ -786,8 +944,14 @@
             even, along = pull(r, f)
             sums = [sums[a] + (even * f[a] + along * r[a]) for a in range(3)]
         for a in range(3):
-            row = jnp.sum(sums[a], axis=0, keepdims=True) * inv_eight_pi + near_ref[a, t : t + 1, :]
-            part_ref[a : a + 1, NPT * t : NPT * (t + 1)] = row[:, 0:NPT]
+            row = jnp.sum(sums[a], axis=0, keepdims=True) * inv_eight_pi
+            cell_ref[a, pl.ds(t, 1), :] = row + near_ref[a, pl.ds(t, 1), :]
+        return carry
+
+    lax.fori_loop(0, CPD, one_cell, 0)
+    for t in range(CPD):
+        for a in range(3):
+            part_ref[a : a + 1, NPT * t : NPT * (t + 1)] = cell_ref[a, t : t + 1, 0:NPT]
     copies = [
         remote(part_ref, held_part.at[k], send_part.at[k], recv_part.at[k], target)
         for k, target in enumerate(mates)
@@ -799,12 +963,12 @@
     out_ref[...] = (part_ref[...] + held_part[1]) + (held_part[0] + held_part[2])
 
 
-def last(points, gathered, far_list, surf, down_inverse, comp, near, npoints):
+def last(points, left, quarter, gathered, far_list, surf, down_inverse, comp, near, npoints):
     dma = pltpu.SemaphoreType.DMA
     return pl.pallas_call(
         last_kernel,
         out_shape=jax.ShapeDtypeStruct((3, npoints), f32),
-        in_specs=[SMEM, VMEM, HBM] + [VMEM] * 4,
+        in_specs=[SMEM, VMEM, VMEM, VMEM, HBM] + [VMEM] * 4,
         out_specs=VMEM,
         scratch_shapes=[
             pltpu.VMEM((FAR, 128), i32),
@@ -815,10 +979,17 @@
             pltpu.VMEM((12, FAR, 128), f32),
             pltpu.VMEM((3, 16, 128), f32),
             pltpu.VMEM((ROWS, 128), f32),
+            pltpu.VMEM((3, 16, 128), f32),
+            pltpu.VMEM((512, 128), f32),
+            pltpu.VMEM((512, 128), f32),
+            pltpu.VMEM((14, EQUIV, 256), f32),
+            pltpu.VMEM((14, EQUIV, 256), f32),
             pltpu.VMEM((ROWS, 128), f32),
-            pltpu.VMEM((2, ROWS, 128), f32),
-            pltpu.VMEM((2 * ROWS, 128), bf16),
+            pltpu.VMEM((48, 128), f32),
+            pltpu.VMEM((2, 48, 128), f32),
+            pltpu.VMEM((ROWS, 256), bf16),
             pltpu.VMEM((CPD, ROWS, WIDE), f32),
+            pltpu.VMEM((3, 8, WIDE), f32),
             pltpu.VMEM((3, npoints), f32),
             pltpu.VMEM((3, 3, npoints), f32),
             dma((2,)),
@@ -830,19 +1001,26 @@
             collective_id=1, has_side_effects=True, vmem_limit_bytes=LIMIT
         ),
         name="last",
-    )(points, gathered, in_hbm(far_list), surf, down_inverse, comp, near)
+    )(points, left, quarter, gathered, in_hbm(far_list), surf, down_inverse, comp, near)
 
 
 def body(displacement, point_leaf, near_list, far_list, stiffness, up_inverse, down_inverse):
     table = surface_table()
     surf = jnp.asarray(np.pad(table, ((0, 0), (0, 5))))
     points = jnp.asarray((inner_radius * table).astype(np.float32).reshape(-1))
-    comp, lists, gathered, lefts, spots, rights = first(
+    whole = np.round(3.0 * table)
+    ones = np.ones((EQUIV, 3), np.float32)
+    square = np.sum(whole * whole, axis=1, keepdims=True)
+    left = np.concatenate([np.repeat(whole, 3, axis=1), ones, ones * square, 0.0 * square], axis=1)
+    left = jnp.asarray(left.astype(np.float32))
+    quarter = inner_radius * table.reshape(4, 14, 3)
+    quarter = jnp.asarray(np.pad(quarter, ((0, 0), (0, 2), (0, 5))).astype(np.float32))
+    comp, lists, gathered, lefts, spots, rights, own_sums = first(
         displacement, point_leaf, near_list, stiffness, surf, up_inverse
     )
-    near = near_field(lists, comp, lefts, spots, rights)
+    near = near_field(lists, comp, lefts, spots, rights, own_sums)
     return last(
-        points, gathered, far_list, surf, down_inverse, comp, near, displacement.shape[1]
+        points, left, quarter, gathered, far_list, surf, down_inverse, comp, near, displacement.shape[1]
     )
 
 

time: 63.2 us -> 58.9 us (0.932); the launches traced: 63.5 us -> 58.3 us
  Pallas kernels: 62.8 us -> 57.5 us
    pallas_call x1, Pallas kernels: 10.5 us -> 7.52 us  [near_field(): pl.pallas_call(near_kernel, out_shape=jax.ShapeDtypeStruct((3, 8, WIDE),...]
    pallas_call x1, Pallas kernels: 21.6 us -> 19.9 us  [last(): pl.pallas_call(last_kernel, out_shape=jax.ShapeDtypeStruct((3, npoints),...]
where the time goes in v3:
time: 58.9 us; the launch traced here: 58.3 us
  Pallas kernels  57.5 us (98%)
  local copies, waits for them, and re-layouts  0.63 us (1%)
    pallas_call x1, Pallas kernels, first(): pl.pallas_call(first_kernel, out_shape=(jax.ShapeDtypeStruct((10, 48, WID...  30.1 us
    pallas_call x1, Pallas kernels, last(): pl.pallas_call(last_kernel, out_shape=jax.ShapeDtypeStruct((3, npoints),...  19.9 us
    pallas_call x1, Pallas kernels, near_field(): pl.pallas_call(near_kernel, out_shape=jax.ShapeDtypeStruct((3, 8, WIDE),...  7.52 us

profile of v3, /device:TPU:1, one launch (start us, length us, event | category | flops | bytes accessed | tf_op | source)
XLA Modules:
  0.0 58.3 jit_solution(14593893674827429587)
XLA Ops:
  0.0 0.0 copy-start.1
  0.0 0.0 copy-start.2
  0.0 0.0 copy-start.3
  0.0 0.0 copy-start.4
  0.0 0.0 copy-start
  0.0 30.1 %first.1 = (f32[10,48,384]{2,1,0:T(8,128)S(1)}, s32[8,128]{1,0:T(8,128)S(1)}, f32[8,8,16,128]{3,2,1,0:T(8,128)S(1)}, bf16[18,80,72]{2,1,0:T(8,128)(2,1)S(1)}, f3...) custom-call(f32[3,1872]{1,0:T(4,128)} %disp_hbm.1, s32[1872]{0:T(1024)} %leaf_hbm.1, ...), custom_call_target="tpu_custom_call" | custom-call | tf_op jit(solution)/shard_map/first/pallas_call | solution.py:555
  30.1 7.5 %near_field.1.near_ref = f32[3,8,384]{2,1,0:T(8,128)S(1)} custom-call(s32[8,128]{1,0:T(8,128)S(1)} %get-tuple-element.14.lists, f32[10,48,384]{2,1,0:T(8,128)S(1)} %get-tuple-element.13.comp_ref, bf16[18,80,72]{2,1,0:T(8,128)(2,1)S(1)} %get-tuple-element.15.lefts, f32[6,3,80,128]{3,2,1,0:T(8,128)S(1)} %get-tuple-element.16.spots, ...), custom_call_target="tpu_custom_call" | custom-call | tf_op jit(solution)/shard_map/near_field/pallas_call | solution.py:657
  37.7 0.0 copy-done.1
  37.7 0.0 copy-done.2
  37.7 0.0 copy-done.3
  37.7 0.0 copy-done.4
  37.7 0.0 copy-done
  37.7 19.9 %last.1 = f32[3,1872]{1,0:T(4,128)S(1)} custom-call(f32[168]{0:T(256)S(1)} %copy-done.4, f32[56,16]{1,0:T(8,128)S(1)} %copy-done.3, f32[4,16,8]{2,1,0:T(8,128)S(1)} %copy-done.2, f32[8,8,16,128]{3,2,1,0:T(8,128)S(1)} %get-tuple-element.12.gat_ref, s32[48,2048]{1,0:T(8,128)} %far_hbm.1, f32[56,8]{1,0:T(8,128)S(1)} %copy-done.1, f32[168,168]{1,0:T(8,128)S(1)} %copy-done, ...), custom_call_target="tpu_custom_call" | custom-call | tf_op jit(solution)/shard_map/last/pallas_call | solution.py:968
  57.6 0.6 %copy.13 = f32[3,1872]{1,0:T(4,128)} copy(f32[3,1872]{1,0:T(4,128)S(1)} %last.1) | data formatting | bytes 44928
Async XLA Ops:
  0.0 37.7 %copy-start.1 = (f32[56,8]{1,0:T(8,128)S(1)}, f32[56,8]{1,0:T(8,128)}, u32[]{:S(2)}) copy-start(f32[56,8]{1,0:T(8,128)} %constant.8.clone.surf_hbm.surf_ref) | copy-start | bytes 5380
  0.0 37.7 %copy-start.2 = (f32[4,16,8]{2,1,0:T(8,128)S(1)}, f32[4,16,8]{2,1,0:T(8,128)}, u32[]{:S(2)}) copy-start(f32[4,16,8]{2,1,0:T(8,128)} %constant.11.clone.quarter_ref) | copy-start | bytes 6148
  0.0 37.7 %copy-start.3 = (f32[56,16]{1,0:T(8,128)S(1)}, f32[56,16]{1,0:T(8,128)}, u32[]{:S(2)}) copy-start(f32[56,16]{1,0:T(8,128)} %constant.10.clone.left_ref) | copy-start | bytes 10756
  0.0 37.7 %copy-start.4 = (f32[168]{0:T(256)S(1)}, f32[168]{0:T(256)}, u32[]{:S(2)}) copy-start(f32[168]{0:T(256)} %constant.9.clone.points) | copy-start | bytes 2020
  0.0 37.7 %copy-start = (f32[168,168]{1,0:T(8,128)S(1)}, f32[168,168]{1,0:T(8,128)}, u32[]{:S(2)}) copy-start(f32[168,168]{1,0:T(8,128)} %inverse_ref.1) | copy-start | bytes 338692

commit v4 on v3

--- a/solution.py
+++ b/solution.py
@@ -21,7 +21,6 @@
 OWNABLE = 3 * CPD
 SHARE = NPT // 4
 SHARE_PAD = 80
-COUNT = 127
 
 inv_eight_pi = 1.0 / (8.0 * math.pi)
 smooth_sq = 0.0625
@@ -77,6 +76,7 @@
 LIMIT = 20 << 20
 HBM = pl.BlockSpec(memory_space=pltpu.HBM)
 DUMMY = CELLS
+TOGETHER = 4
 BATCH = 6
 PARTS = 2
 EARLY = 5
@@ -315,43 +315,46 @@
     left_second = (slot < 18) & (slot_turn >= 3) & (slot_turn < 5) | (slot == 19)
     row32 = iota((32, WIDE), 0)
 
-    def one_own(t, carry):
+    def one_own(t):
         rel = comp_ref[REL, pl.ds(t, 1), :]
         px, py, pz = [comp_ref[PX + a, pl.ds(t, 1), :] for a in range(3)]
         lowest = jnp.min(jnp.where(rel >= 0.0, rel, 1e9), axis=1, keepdims=True)
         owner = jnp.floor(lowest * (1.0 / PER_OWNER))
         py4, pz4 = py - 4.0, pz - 4.0
-        extra = iota((8, WIDE), 0)
-        place = jnp.where(extra == 0, px, jnp.where(extra == 1, py, jnp.where(extra == 2, pz, rel)))
-        top, middle, low = thirds(place)
-        spot = dot_nt(pick16, top.astype(bf16)) + (
+        rows = []
+        for w in range(3):
+            px4 = px - (4.0 * (owner + float(w - 1)) + 2.0)
+            square = (px4 * px4 + py4 * py4) + pz4 * pz4
+            rows.append(
+                jnp.where(
+                    row32 < 6,
+                    px4,
+                    jnp.where(row32 < 12, py4, jnp.where(row32 < 18, pz4, square)),
+                )
+            )
+        place = jnp.where(row32 == 0, px, jnp.where(row32 == 1, py, jnp.where(row32 == 2, pz, rel)))
+        top, middle, low = thirds(jnp.concatenate([*rows, place], axis=0))
+        found = dot_nt(pick16, top.astype(bf16)) + (
             dot_nt(pick16, middle.astype(bf16)) + dot_nt(pick16, low.astype(bf16))
         )
         for a in range(3):
-            spots_ref[t, a] = jnp.broadcast_to(spot[:, a : a + 1], (SHARE_PAD, 128))
-        leaf_at = (spot[:, 3:4] - lowest).astype(i32)
+            spots_ref[t, a] = jnp.broadcast_to(found[:, 96 + a : 97 + a], (SHARE_PAD, 128))
+        leaf_at = (found[:, 99:100] - lowest).astype(i32)
         matched = (slot - (FEATURES + 8 * t) == leaf_at) & (leaf_at >= 0) & (leaf_at < 3)
         for w in range(3):
-            px4 = px - (4.0 * (owner + float(w - 1)) + 2.0)
-            square = (px4 * px4 + py4 * py4) + pz4 * pz4
-            rows = jnp.where(
-                row32 < 6,
-                px4,
-                jnp.where(row32 < 12, py4, jnp.where(row32 < 18, pz4, square)),
-            )
-            rows = jnp.concatenate([rows, jnp.zeros((96, WIDE), f32)], axis=0)
-            top, middle, low = thirds(rows)
-            value = dot_nt(pick16, top.astype(bf16)) + (
-                dot_nt(pick16, middle.astype(bf16)) + dot_nt(pick16, low.astype(bf16))
-            )
+            value = pltpu.roll(found, 128 - 32 * w, 1) if w else found
             top, middle, low = thirds(value)
             chosen = jnp.where(left_first, top, jnp.where(left_second, middle, low))
             chosen = jnp.where((slot >= 21) & (slot < 24), 1.0, chosen)
             chosen = jnp.where(slot >= FEATURES, jnp.where(matched, 1.0, 0.0), chosen)
             lefts_ref[3 * t + w] = chosen[:, 0:DEPTH].astype(bf16)
+
+    def two_own(index, carry):
+        one_own(2 * index)
+        one_own(2 * index + 1)
         return carry
 
-    lax.fori_loop(0, CPD, one_own, 0)
+    lax.fori_loop(0, CPD // 2, two_own, 0)
     for a in range(3):
         wide[a] = jnp.broadcast_to(outer_radius * surf_ref[:, a : a + 1], (EQUIV, 128))
 
@@ -439,14 +442,22 @@
         table = table + jnp.where(lane == t, flag, 0.0)
     rank = dot(before, table)
     count = jnp.sum(table, axis=0, keepdims=True)
-    lane_row = iota((1, 128), 1)
+    lane_row = iota((1, 128), 1).astype(f32)
     lists_ref[...] = jnp.zeros_like(lists_ref)
+    lines = [jnp.zeros((1, 128), f32) for _ in range(2)]
+    ahead = jnp.zeros((1, 1), f32)
     for t, flag in enumerate(flags):
-        hit = (rank[:, t : t + 1] == lane.astype(f32)) & (flag > 0.0)
-        line = jnp.sum(jnp.where(hit, which, 0.0), axis=0, keepdims=True)
-        line = jnp.where(lane_row.astype(f32) >= count[:, t : t + 1], float(DUMMY), line)
-        line = jnp.where(lane_row == COUNT, count[:, t : t + 1], line)
-        lists_ref[t : t + 1, :] = line.astype(i32)
+        spot = rank[:, t : t + 1] + ahead
+        for half in range(2):
+            hit = (spot == lane.astype(f32) + 128.0 * half) & (flag > 0.0)
+            lines[half] = lines[half] + jnp.sum(
+                jnp.where(hit, which + 64.0 * t, 0.0), axis=0, keepdims=True
+            )
+        ahead = ahead + count[:, t : t + 1]
+    for half in range(2):
+        line = jnp.where(lane_row + 128.0 * half >= ahead, float(DUMMY), lines[half])
+        lists_ref[half : half + 1, :] = line.astype(i32)
+    lists_ref[2:3, :] = jnp.broadcast_to(ahead, (1, 128)).astype(i32)
     square = iota((48, 128), 0) == lane
     line = jnp.sum(jnp.where(square, owner, 0.0), axis=0, keepdims=True)
     lists_ref[7:8, :] = line.astype(i32)
@@ -614,30 +625,27 @@
 def near_kernel(lists, comp_ref, lefts, spots, rights, own_sums, out_ref, even_pairs, odd_pairs, sums):
     portion = lax.axis_index("leaf")
 
-    def multiply(t, index, products):
-        c = lists[t, index]
+    def pair(index):
+        code = lists[index >> 7, index & 127]
+        return code >> 6, code & 63
+
+    def multiply(index, products):
+        t, c = pair(index)
         w = jnp.clip(lists[7, c] - lists[7, t] + 1, 0, 2)
         products[...] = dot(lefts[3 * t + w], rights[c])
 
     sums[...] = own_sums[...]
-    multiply(0, 0, even_pairs)
-
-    def one_target(t, carry):
-        steps = jnp.maximum((lists[t, COUNT] + 1) // 2, 1)
-
-        def two_pairs(index, carry):
-            multiply(t, 2 * index + 1, odd_pairs)
-            add_pair(comp_ref, sums, t, lists[t, 2 * index], even_pairs)
-            ends = index + 1 == steps
-            after = jnp.where(ends, jnp.minimum(t + 1, CPD - 1), t)
-            multiply(after, jnp.where(ends, 0, 2 * index + 2), even_pairs)
-            add_pair(comp_ref, sums, t, lists[t, 2 * index + 1], odd_pairs)
-            return carry
-
-        lax.fori_loop(0, steps, two_pairs, 0)
+    multiply(0, even_pairs)
+
+    def some_pairs(index, carry):
+        for k in range(TOGETHER):
+            now, after = (odd_pairs, even_pairs) if k % 2 else (even_pairs, odd_pairs)
+            at = TOGETHER * index + k
+            multiply(at + 1, after)
+            add_pair(comp_ref, sums, *pair(at), now)
         return carry
 
-    lax.fori_loop(0, CPD, one_target, 0)
+    lax.fori_loop(0, (lists[2, 0] + (TOGETHER - 1)) // TOGETHER, some_pairs, 0)
     pick_row, pick_lane = iota((SHARE_PAD, WIDE), 0), iota((SHARE_PAD, WIDE), 1)
     pick = (pick_lane == pick_row + SHARE * portion) & (pick_row < SHARE)
 
@@ -672,7 +680,6 @@
 def far_part(
     left_ref,
     quarter_ref,
-    points,
     gat_ref,
     far_ref,
     far_load,
@@ -738,7 +745,7 @@
     mids[1, 0:12, :] = (2 * (((target >> 2) & 3) - ((merged >> 2) & 3))).astype(f32)
     mids[2, 0:12, :] = (2 * ((target & 3) - (merged & 3))).astype(f32)
 
-    def one_gather(index, carry):
+    def gather_two(index):
         first = sources[pl.ds(2 * index, 1), :]
         second = sources[pl.ds(2 * index + 1, 1), :]
         wanted = jnp.concatenate([first, second], axis=1)
@@ -749,9 +756,13 @@
         value = found[0:48] + found[48:96]
         pushes[2 * index] = value[:, 0:128]
         pushes[2 * index + 1] = value[:, 128:256]
+
+    def some_gathers(index, carry):
+        for k in range(3):
+            gather_two(3 * index + k)
         return carry
 
-    lax.fori_loop(0, 6, one_gather, 0)
+    lax.fori_loop(0, 2, some_gathers, 0)
     total[...] = jnp.zeros_like(total)
 
     left = left_ref[...].astype(bf16)
@@ -789,7 +800,7 @@
         sums = [[jnp.zeros((8, 128), f32) for _ in range(4)] for _ in range(groups)]
         for j in range(14):
             f = [pushes[index, 16 * a + j : 16 * a + j + 1, :] for a in range(3)]
-            shift = [points[3 * (14 * portion + j) + a] for a in range(3)]
+            shift = [quarter[a, j : j + 1, :] for a in range(3)]
             for g in range(groups):
                 at = slice(8 * g, 8 * g + 8)
                 shifted = blocks[j, at, 0:128]
@@ -826,7 +837,6 @@
 
 
 def last_kernel(
-    points,
     left_ref,
     quarter_ref,
     gat_ref,
@@ -874,7 +884,6 @@
     far_part(
         left_ref,
         quarter_ref,
-        points,
         gat_ref,
         far_ref,
         far_load,
@@ -934,7 +943,7 @@
 
     lax.fori_loop(0, 2, three_cells, 0)
 
-    def one_cell(t, carry):
+    def one_cell(t):
         d = [comp_ref[DX + a, pl.ds(t, 1), :] for a in range(3)]
         sums = [jnp.zeros((8, WIDE), f32) for _ in range(3)]
         for g in range(EQUIV // 8):
@@ -946,9 +955,13 @@
         for a in range(3):
             row = jnp.sum(sums[a], axis=0, keepdims=True) * inv_eight_pi
             cell_ref[a, pl.ds(t, 1), :] = row + near_ref[a, pl.ds(t, 1), :]
+
+    def two_cells(index, carry):
+        one_cell(2 * index)
+        one_cell(2 * index + 1)
         return carry
 
-    lax.fori_loop(0, CPD, one_cell, 0)
+    lax.fori_loop(0, CPD // 2, two_cells, 0)
     for t in range(CPD):
         for a in range(3):
             part_ref[a : a + 1, NPT * t : NPT * (t + 1)] = cell_ref[a, t : t + 1, 0:NPT]
@@ -963,12 +976,12 @@
     out_ref[...] = (part_ref[...] + held_part[1]) + (held_part[0] + held_part[2])
 
 
-def last(points, left, quarter, gathered, far_list, surf, down_inverse, comp, near, npoints):
+def last(left, quarter, gathered, far_list, surf, down_inverse, comp, near, npoints):
     dma = pltpu.SemaphoreType.DMA
     return pl.pallas_call(
         last_kernel,
         out_shape=jax.ShapeDtypeStruct((3, npoints), f32),
-        in_specs=[SMEM, VMEM, VMEM, VMEM, HBM] + [VMEM] * 4,
+        in_specs=[VMEM, VMEM, VMEM, HBM] + [VMEM] * 4,
         out_specs=VMEM,
         scratch_shapes=[
             pltpu.VMEM((FAR, 128), i32),
@@ -1001,13 +1014,12 @@
             collective_id=1, has_side_effects=True, vmem_limit_bytes=LIMIT
         ),
         name="last",
-    )(points, left, quarter, gathered, in_hbm(far_list), surf, down_inverse, comp, near)
+    )(left, quarter, gathered, in_hbm(far_list), surf, down_inverse, comp, near)
 
 
 def body(displacement, point_leaf, near_list, far_list, stiffness, up_inverse, down_inverse):
     table = surface_table()
     surf = jnp.asarray(np.pad(table, ((0, 0), (0, 5))))
-    points = jnp.asarray((inner_radius * table).astype(np.float32).reshape(-1))
     whole = np.round(3.0 * table)
     ones = np.ones((EQUIV, 3), np.float32)
     square = np.sum(whole * whole, axis=1, keepdims=True)
@@ -1020,7 +1032,7 @@
     )
     near = near_field(lists, comp, lefts, spots, rights, own_sums)
     return last(
-        points, left, quarter, gathered, far_list, surf, down_inverse, comp, near, displacement.shape[1]
+        left, quarter, gathered, far_list, surf, down_inverse, comp, near, displacement.shape[1]
     )
 
 

time: 58.9 us -> 55.1 us (0.935)
  Pallas kernels: 57.5 us -> 54.1 us
    pallas_call x1, Pallas kernels: 7.52 us -> 5.69 us  [near_field(): pl.pallas_call(near_kernel, out_shape=jax.ShapeDtypeStruct((3, 8, WIDE),...]
    pallas_call x1, Pallas kernels: 19.9 us -> 18.4 us  [last(): pl.pallas_call(last_kernel, out_shape=jax.ShapeDtypeStruct((3, npoints),...]
where the time goes in v4:
time: 55.1 us; the launch traced here: 54.8 us
  Pallas kernels  54.1 us (98%)
  local copies, waits for them, and re-layouts  0.63 us (1%)
    pallas_call x1, Pallas kernels, first(): pl.pallas_call(first_kernel, out_shape=(jax.ShapeDtypeStruct((10, 48, WID...  30.1 us
    pallas_call x1, Pallas kernels, last(): pl.pallas_call(last_kernel, out_shape=jax.ShapeDtypeStruct((3, npoints),...  18.4 us
    pallas_call x1, Pallas kernels, near_field(): pl.pallas_call(near_kernel, out_shape=jax.ShapeDtypeStruct((3, 8, WIDE),...  5.69 us

profile of v4, /device:TPU:1, one launch (start us, length us, event | category | flops | bytes accessed | tf_op | source)
XLA Modules:
  0.0 54.8 jit_solution(8440911978855413927)
XLA Ops:
  0.0 0.0 copy-start.1
  0.0 0.0 copy-start.2
  0.0 0.0 copy-start.3
  0.0 0.0 copy-start
  0.0 30.1 %first.1 = (f32[10,48,384]{2,1,0:T(8,128)S(1)}, s32[8,128]{1,0:T(8,128)S(1)}, f32[8,8,16,128]{3,2,1,0:T(8,128)S(1)}, bf16[18,80,72]{2,1,0:T(8,128)(2,1)S(1)}, f3...) custom-call(f32[3,1872]{1,0:T(4,128)} %disp_hbm.1, s32[1872]{0:T(1024)} %leaf_hbm.1, ...), custom_call_target="tpu_custom_call" | custom-call | tf_op jit(solution)/shard_map/first/pallas_call | solution.py:566
  30.1 5.7 %near_field.1.near_ref = f32[3,8,384]{2,1,0:T(8,128)S(1)} custom-call(s32[8,128]{1,0:T(8,128)S(1)} %get-tuple-element.14.lists, f32[10,48,384]{2,1,0:T(8,128)S(1)} %get-tuple-element.13.comp_ref, bf16[18,80,72]{2,1,0:T(8,128)(2,1)S(1)} %get-tuple-element.15.lefts, f32[6,3,80,128]{3,2,1,0:T(8,128)S(1)} %get-tuple-element.16.spots, ...), custom_call_target="tpu_custom_call" | custom-call | tf_op jit(solution)/shard_map/near_field/pallas_call | solution.py:665
  35.8 0.0 copy-done.1
  35.8 0.0 copy-done.2
  35.8 0.0 copy-done.3
  35.8 0.0 copy-done
  35.9 18.4 %last.1 = f32[3,1872]{1,0:T(4,128)S(1)} custom-call(f32[56,16]{1,0:T(8,128)S(1)} %copy-done.3, f32[4,16,8]{2,1,0:T(8,128)S(1)} %copy-done.2, f32[8,8,16,128]{3,2,1,0:T(8,128)S(1)} %get-tuple-element.12.gat_ref, s32[48,2048]{1,0:T(8,128)} %far_hbm.1, f32[56,8]{1,0:T(8,128)S(1)} %copy-done.1, f32[168,168]{1,0:T(8,128)S(1)} %copy-done, ...), custom_call_target="tpu_custom_call" | custom-call | tf_op jit(solution)/shard_map/last/pallas_call | solution.py:981
  54.2 0.6 %copy.12 = f32[3,1872]{1,0:T(4,128)} copy(f32[3,1872]{1,0:T(4,128)S(1)} %last.1) | data formatting | bytes 44928
Async XLA Ops:
  0.0 35.8 %copy-start.1 = (f32[56,8]{1,0:T(8,128)S(1)}, f32[56,8]{1,0:T(8,128)}, u32[]{:S(2)}) copy-start(f32[56,8]{1,0:T(8,128)} %constant.6.clone.surf_hbm.surf_ref) | copy-start | bytes 5380
  0.0 35.8 %copy-start.2 = (f32[4,16,8]{2,1,0:T(8,128)S(1)}, f32[4,16,8]{2,1,0:T(8,128)}, u32[]{:S(2)}) copy-start(f32[4,16,8]{2,1,0:T(8,128)} %constant.8.clone.quarter_ref) | copy-start | bytes 6148
  0.0 35.8 %copy-start.3 = (f32[56,16]{1,0:T(8,128)S(1)}, f32[56,16]{1,0:T(8,128)}, u32[]{:S(2)}) copy-start(f32[56,16]{1,0:T(8,128)} %constant.7.clone.left_ref) | copy-start | bytes 10756
  0.0 35.8 %copy-start = (f32[168,168]{1,0:T(8,128)S(1)}, f32[168,168]{1,0:T(8,128)}, u32[]{:S(2)}) copy-start(f32[168,168]{1,0:T(8,128)} %inverse_ref.1) | copy-start | bytes 338692

commit v5 on v4

--- a/solution.py
+++ b/solution.py
@@ -79,8 +79,7 @@
 TOGETHER = 4
 BATCH = 6
 PARTS = 2
-EARLY = 5
-MIDDLE = 3
+STEPS = (0, 1, 7, 2, 6, 3, 5, 4)
 
 
 def thirds(value):
@@ -426,6 +425,40 @@
     ]
     for copy in z_copies:
         copy.start()
+    y_copies, c_copies = [], []
+
+    def send_along_y(source, where, order):
+        for side, target in enumerate(y_targets):
+            index = 3 * order + side
+            copy = remote(source, gat_ref.at[row, where], y_send.at[index], y_recv.at[index], target)
+            copy.start()
+            y_copies.append(copy)
+
+    def pass_on(source, at, where, index):
+        copy = remote(source, gat_ref.at[at, where], c_send.at[index], c_recv.at[index], c_target)
+        copy.start()
+        c_copies.append(copy)
+
+    def take_z(orders):
+        for order in orders:
+            k = STEPS[order]
+            where = lax.rem(z - k + 8, 8)
+            z_copies[k - 1].wait_recv()
+            place = gat_ref.at[row, where]
+            send_along_y(place, where, order)
+            pass_on(place, row, where, order)
+
+    def take_y(orders):
+        for order in orders:
+            where = lax.rem(z - STEPS[order] + 8, 8)
+            for side in range(3):
+                index = 3 * order + side
+                y_copies[index].wait_recv()
+                at = core * 4 + lax.rem(y - side + 3, 4)
+                pass_on(gat_ref.at[at, where], at, where, 8 + index)
+
+    send_along_y(block_ref, z, 0)
+    pass_on(block_ref, row, z, 0)
 
     low = jnp.floor(first * (1.0 / 16.0))
     high = jnp.floor(last * (1.0 / 16.0))
@@ -521,38 +554,18 @@
 
     sums_ref[...] = jnp.zeros_like(sums_ref)
     rights_ref[DUMMY] = jnp.where(iota((DEPTH, 2 * WIDE), 0) == 21, FAR_AWAY, 0.0).astype(bf16)
-    lax.fori_loop(0, EARLY, some_sources, 0)
-
+    lax.fori_loop(0, 3, some_sources, 0)
+    take_z((1, 2))
+    lax.fori_loop(3, 5, some_sources, 0)
     own.wait()
-    y_copies, c_copies = [], []
-
-    def pass_on(at, where, index):
-        place = gat_ref.at[at, where]
-        copy = remote(place, place, c_send.at[index], c_recv.at[index], c_target)
-        copy.start()
-        c_copies.append(copy)
-
-    for order, k in enumerate((0, 1, 7, 2, 6, 3, 5, 4)):
-        where = lax.rem(z - k + 8, 8)
-        if k:
-            z_copies[k - 1].wait_recv()
-        place = gat_ref.at[row, where]
-        for side, target in enumerate(y_targets):
-            index = 3 * order + side
-            copy = remote(place, place, y_send.at[index], y_recv.at[index], target)
-            copy.start()
-            y_copies.append(copy)
-        pass_on(row, where, order)
-    lax.fori_loop(EARLY, CELLS // BATCH, some_sources, 0)
+    take_z(range(3, 8))
+    lax.fori_loop(5, CELLS // BATCH, some_sources, 0)
     multiply_own(0, 0, even_pairs)
-    lax.fori_loop(0, MIDDLE, own_target, 0)
-    for order, k in enumerate((0, 1, 7, 2, 6, 3, 5, 4)):
-        where = lax.rem(z - k + 8, 8)
-        for side in range(3):
-            index = 3 * order + side
-            y_copies[index].wait_recv()
-            pass_on(core * 4 + lax.rem(y - side + 3, 4), where, 8 + index)
-    lax.fori_loop(MIDDLE, CPD, own_target, 0)
+    lax.fori_loop(0, 2, own_target, 0)
+    take_y(range(3))
+    lax.fori_loop(2, 4, own_target, 0)
+    take_y(range(3, 8))
+    lax.fori_loop(4, CPD, own_target, 0)
     for copy in (*z_copies, *y_copies):
         copy.wait_send()
     for copy in c_copies:

time: 55.1 us -> 54.3 us (0.985)
  Pallas kernels: 54.1 us -> 53 us
    pallas_call x1, Pallas kernels: 18.4 us -> 16.8 us  [last(): pl.pallas_call(last_kernel, out_shape=jax.ShapeDtypeStruct((3, npoints),...]
    pallas_call x1, Pallas kernels: 5.69 us -> 6.65 us  [near_field(): pl.pallas_call(near_kernel, out_shape=jax.ShapeDtypeStruct((3, 8, WIDE),...]
where the time goes in v5:
time: 54.3 us; the launch traced here: 53.7 us
  Pallas kernels  53 us (98%)
  local copies, waits for them, and re-layouts  0.63 us (1%)
    pallas_call x1, Pallas kernels, first(): pl.pallas_call(first_kernel, out_shape=(jax.ShapeDtypeStruct((10, 48, WID...  29.6 us
    pallas_call x1, Pallas kernels, last(): pl.pallas_call(last_kernel, out_shape=jax.ShapeDtypeStruct((3, npoints),...  16.8 us
    pallas_call x1, Pallas kernels, near_field(): pl.pallas_call(near_kernel, out_shape=jax.ShapeDtypeStruct((3, 8, WIDE),...  6.65 us

profile of v5, /device:TPU:1, one launch (start us, length us, event | category | flops | bytes accessed | tf_op | source)
XLA Modules:
  0.0 53.7 jit_solution(3577755650156181929)
XLA Ops:
  0.0 0.0 copy-start.1
  0.0 0.0 copy-start.2
  0.0 0.0 copy-start.3
  0.0 0.0 copy-start
  0.0 29.6 %first.1 = (f32[10,48,384]{2,1,0:T(8,128)S(1)}, s32[8,128]{1,0:T(8,128)S(1)}, f32[8,8,16,128]{3,2,1,0:T(8,128)S(1)}, bf16[18,80,72]{2,1,0:T(8,128)(2,1)S(1)}, f3...) custom-call(f32[3,1872]{1,0:T(4,128)} %disp_hbm.1, s32[1872]{0:T(1024)} %leaf_hbm.1, ...), custom_call_target="tpu_custom_call" | custom-call | tf_op jit(solution)/shard_map/first/pallas_call | solution.py:579
  29.6 6.6 %near_field.1.near_ref = f32[3,8,384]{2,1,0:T(8,128)S(1)} custom-call(s32[8,128]{1,0:T(8,128)S(1)} %get-tuple-element.14.lists, f32[10,48,384]{2,1,0:T(8,128)S(1)} %get-tuple-element.13.comp_ref, bf16[18,80,72]{2,1,0:T(8,128)(2,1)S(1)} %get-tuple-element.15.lefts, f32[6,3,80,128]{3,2,1,0:T(8,128)S(1)} %get-tuple-element.16.spots, ...), custom_call_target="tpu_custom_call" | custom-call | tf_op jit(solution)/shard_map/near_field/pallas_call | solution.py:678
  36.3 0.0 copy-done.1
  36.3 0.0 copy-done.2
  36.3 0.0 copy-done.3
  36.3 0.0 copy-done
  36.3 16.8 %last.1 = f32[3,1872]{1,0:T(4,128)S(1)} custom-call(f32[56,16]{1,0:T(8,128)S(1)} %copy-done.3, f32[4,16,8]{2,1,0:T(8,128)S(1)} %copy-done.2, f32[8,8,16,128]{3,2,1,0:T(8,128)S(1)} %get-tuple-element.12.gat_ref, s32[48,2048]{1,0:T(8,128)} %far_hbm.1, f32[56,8]{1,0:T(8,128)S(1)} %copy-done.1, f32[168,168]{1,0:T(8,128)S(1)} %copy-done, ...), custom_call_target="tpu_custom_call" | custom-call | tf_op jit(solution)/shard_map/last/pallas_call | solution.py:994
  53.1 0.6 %copy.12 = f32[3,1872]{1,0:T(4,128)} copy(f32[3,1872]{1,0:T(4,128)S(1)} %last.1) | data formatting | bytes 44928
Async XLA Ops:
  0.0 36.3 %copy-start.1 = (f32[56,8]{1,0:T(8,128)S(1)}, f32[56,8]{1,0:T(8,128)}, u32[]{:S(2)}) copy-start(f32[56,8]{1,0:T(8,128)} %constant.6.clone.surf_hbm.surf_ref) | copy-start | bytes 5380
  0.0 36.3 %copy-start.2 = (f32[4,16,8]{2,1,0:T(8,128)S(1)}, f32[4,16,8]{2,1,0:T(8,128)}, u32[]{:S(2)}) copy-start(f32[4,16,8]{2,1,0:T(8,128)} %constant.8.clone.quarter_ref) | copy-start | bytes 6148
  0.0 36.3 %copy-start.3 = (f32[56,16]{1,0:T(8,128)S(1)}, f32[56,16]{1,0:T(8,128)}, u32[]{:S(2)}) copy-start(f32[56,16]{1,0:T(8,128)} %constant.7.clone.left_ref) | copy-start | bytes 10756
  0.0 36.3 %copy-start = (f32[168,168]{1,0:T(8,128)S(1)}, f32[168,168]{1,0:T(8,128)}, u32[]{:S(2)}) copy-start(f32[168,168]{1,0:T(8,128)} %inverse_ref.1) | copy-start | bytes 338692

commit v6 on v5

--- a/solution.py
+++ b/solution.py
@@ -76,7 +76,7 @@
 LIMIT = 20 << 20
 HBM = pl.BlockSpec(memory_space=pltpu.HBM)
 DUMMY = CELLS
-TOGETHER = 4
+TOGETHER = 6
 BATCH = 6
 PARTS = 2
 STEPS = (0, 1, 7, 2, 6, 3, 5, 4)
@@ -876,6 +876,7 @@
     packed_local,
     held_local,
     factors,
+    member_ref,
     spread_ref,
     cell_ref,
     part_ref,
@@ -928,6 +929,11 @@
     ]
     for copy in copies:
         copy.start()
+    for t in range(CPD):
+        rel = comp_ref[REL, t : t + 1, :].astype(i32) - 3 * PER_OWNER
+        member = (iota((128, WIDE), 0) == rel).astype(f32).astype(bf16)
+        member_ref[t, 0:128, :] = member
+        member_ref[t, 128:256, :] = member
     for copy in copies:
         copy.wait()
     lane = iota((48, 128), 1) // PER_OWNER
@@ -945,16 +951,10 @@
         factors[48 * k : 48 * k + rows, 128:256] = low
 
     def spread_out(t):
-        rel = comp_ref[REL, pl.ds(t, 1), :].astype(i32) - 3 * PER_OWNER
-        member = (iota((128, WIDE), 0) == rel).astype(f32).astype(bf16)
-        spread_ref[t] = dot(factors[...], jnp.concatenate([member, member], axis=0))
-
-    def three_cells(index, carry):
-        for k in range(3):
-            spread_out(3 * index + k)
-        return carry
-
-    lax.fori_loop(0, 2, three_cells, 0)
+        spread_ref[t] = dot(factors[...], member_ref[t])
+
+    for t in range(CPD):
+        spread_out(t)
 
     def one_cell(t):
         d = [comp_ref[DX + a, pl.ds(t, 1), :] for a in range(3)]
@@ -1014,6 +1014,7 @@
             pltpu.VMEM((48, 128), f32),
             pltpu.VMEM((2, 48, 128), f32),
             pltpu.VMEM((ROWS, 256), bf16),
+            pltpu.VMEM((CPD, 256, WIDE), bf16),
             pltpu.VMEM((CPD, ROWS, WIDE), f32),
             pltpu.VMEM((3, 8, WIDE), f32),
             pltpu.VMEM((3, npoints), f32),

time: 54.3 us -> 54 us (level)
    pallas_call x1, Pallas kernels: 6.65 us -> 6.04 us  [near_field(): pl.pallas_call(near_kernel, out_shape=jax.ShapeDtypeStruct((3, 8, WIDE),...]
where the time goes in v6:
time: 54 us; the launch traced here: 53.3 us
  Pallas kernels  52.6 us (97%)
  local copies, waits for them, and re-layouts  0.63 us (1%)
    pallas_call x1, Pallas kernels, first(): pl.pallas_call(first_kernel, out_shape=(jax.ShapeDtypeStruct((10, 48, WID...  29.6 us
    pallas_call x1, Pallas kernels, last(): pl.pallas_call(last_kernel, out_shape=jax.ShapeDtypeStruct((3, npoints),...  16.9 us
    pallas_call x1, Pallas kernels, near_field(): pl.pallas_call(near_kernel, out_shape=jax.ShapeDtypeStruct((3, 8, WIDE),...  6.04 us

profile of v6, /device:TPU:1, one launch (start us, length us, event | category | flops | bytes accessed | tf_op | source)
XLA Modules:
  0.0 53.3 jit_solution(10075122273180616316)
XLA Ops:
  0.0 0.0 copy-start.1
  0.0 0.0 copy-start.2
  0.0 0.0 copy-start.3
  0.0 0.0 copy-start
  0.0 29.6 %first.1 = (f32[10,48,384]{2,1,0:T(8,128)S(1)}, s32[8,128]{1,0:T(8,128)S(1)}, f32[8,8,16,128]{3,2,1,0:T(8,128)S(1)}, bf16[18,80,72]{2,1,0:T(8,128)(2,1)S(1)}, f3...) custom-call(f32[3,1872]{1,0:T(4,128)} %disp_hbm.1, s32[1872]{0:T(1024)} %leaf_hbm.1, ...), custom_call_target="tpu_custom_call" | custom-call | tf_op jit(solution)/shard_map/first/pallas_call | solution.py:579
  29.6 6.0 %near_field.1.near_ref = f32[3,8,384]{2,1,0:T(8,128)S(1)} custom-call(s32[8,128]{1,0:T(8,128)S(1)} %get-tuple-element.14.lists, f32[10,48,384]{2,1,0:T(8,128)S(1)} %get-tuple-element.13.comp_ref, bf16[18,80,72]{2,1,0:T(8,128)(2,1)S(1)} %get-tuple-element.15.lefts, f32[6,3,80,128]{3,2,1,0:T(8,128)S(1)} %get-tuple-element.16.spots, ...), custom_call_target="tpu_custom_call" | custom-call | tf_op jit(solution)/shard_map/near_field/pallas_call | solution.py:678
  35.7 0.0 copy-done.1
  35.7 0.0 copy-done.2
  35.7 0.0 copy-done.3
  35.7 0.0 copy-done
  35.7 16.9 %last.1 = f32[3,1872]{1,0:T(4,128)S(1)} custom-call(f32[56,16]{1,0:T(8,128)S(1)} %copy-done.3, f32[4,16,8]{2,1,0:T(8,128)S(1)} %copy-done.2, f32[8,8,16,128]{3,2,1,0:T(8,128)S(1)} %get-tuple-element.12.gat_ref, s32[48,2048]{1,0:T(8,128)} %far_hbm.1, f32[56,8]{1,0:T(8,128)S(1)} %copy-done.1, f32[168,168]{1,0:T(8,128)S(1)} %copy-done, ...), custom_call_target="tpu_custom_call" | custom-call | tf_op jit(solution)/shard_map/last/pallas_call | solution.py:994
  52.6 0.6 %copy.12 = f32[3,1872]{1,0:T(4,128)} copy(f32[3,1872]{1,0:T(4,128)S(1)} %last.1) | data formatting | bytes 44928
Async XLA Ops:
  0.0 35.7 %copy-start.1 = (f32[56,8]{1,0:T(8,128)S(1)}, f32[56,8]{1,0:T(8,128)}, u32[]{:S(2)}) copy-start(f32[56,8]{1,0:T(8,128)} %constant.6.clone.surf_hbm.surf_ref) | copy-start | bytes 5380
  0.0 35.7 %copy-start.2 = (f32[4,16,8]{2,1,0:T(8,128)S(1)}, f32[4,16,8]{2,1,0:T(8,128)}, u32[]{:S(2)}) copy-start(f32[4,16,8]{2,1,0:T(8,128)} %constant.8.clone.quarter_ref) | copy-start | bytes 6148
  0.0 35.7 %copy-start.3 = (f32[56,16]{1,0:T(8,128)S(1)}, f32[56,16]{1,0:T(8,128)}, u32[]{:S(2)}) copy-start(f32[56,16]{1,0:T(8,128)} %constant.7.clone.left_ref) | copy-start | bytes 10756
  0.0 35.7 %copy-start = (f32[168,168]{1,0:T(8,128)S(1)}, f32[168,168]{1,0:T(8,128)}, u32[]{:S(2)}) copy-start(f32[168,168]{1,0:T(8,128)} %inverse_ref.1) | copy-start | bytes 338692
